TPU v7x, 128 devices: a whole 4x4x4 slice. The times are simulated.
128 devices in a mesh: shard: 128 (over z, x, y, core).
Axes of the slice: x: 4, y: 4, z: 4, core: 2. Of those that a mesh axis runs over, the one named last changes fastest.
Arguments:
- data_t: bfloat16 [8192, 32768], P('shard'), may hold values from -0.25 to 0.25
- labels: int32 [32768], replicated, may hold values from -1 to 1, as said below
- sample_weight: float32 [32768], replicated, may hold values from 0.1 to 4
- w_start: float32 [8192], P('shard'), may hold values from -10 to 10
- alpha_start: float32 [32768], P('shard'), may hold values from 0 to 1
- visit_order: int32 [256, 128], P('shard'), may hold values from 0 to 127, each once within a row
Outputs:
- weights_out: float32 [8192], P('shard')
- alpha_final: float32 [32768], P('shard')
- objective: float32 [], replicated
Inputs may be any that keep to these rules, and one draw needn't show every extreme that they name: `labels`: each label is -1 or +1. `visit_order`: each row is a permutation of 0 to 127.
All inputs are finite; a program needn't handle non-finite values.
Results may differ from a plain program's by a relative error of at most 0.0047.
Values may be sent and summed in bfloat16 or wider, within the bound.
A program may use at most 64 MiB of HBM per device.

v0:
```python
import jax
import jax.numpy as jnp
from jax import lax
from jax.sharding import Mesh
from jax.sharding import PartitionSpec as P

GROUP = 16
SHARD = ("shard_0", "shard_1", "shard_2", "shard_3")


def cut_along(array, dim, size):
    before, after = (array.shape[:dim], array.shape[dim + 1 :])
    return jnp.moveaxis(array.reshape(*before, size, -1, *after), dim, 0)


def sum_at_owner(array, axis, dim):
    size = lax.axis_size(axis)
    pieces = lax.all_to_all(cut_along(array, dim, size), axis, 0, 0, tiled=True)
    return jnp.sum(pieces, axis=0)


def sum_in_two_steps(array, axes, dim):
    far, near = axes
    own = sum_at_owner(cut_along(array, dim, lax.axis_size(far)), near, dim + 1)
    return jnp.sum(lax.all_to_all(own, far, 0, 0, tiled=True), axis=0)


def padded_to(lines, size):
    spare = -lines.shape[0] % size
    if not spare:
        return lines
    return jnp.concatenate([lines, jnp.zeros((spare, *lines.shape[1:]), lines.dtype)])


def from_everyone(array, axis):
    size = lax.axis_size(axis)
    return lax.all_to_all(
        jnp.broadcast_to(array[None], (size, *array.shape)), axis, 0, 0, tiled=True
    )


def laid_out(pieces, dim):
    shape = list(pieces.shape[1:])
    shape[dim] *= pieces.shape[0]
    return jnp.moveaxis(pieces, 0, dim).reshape(shape)


def whole_of(array, axes, dim):
    far, near = axes
    first = from_everyone(array, far)
    pieces = jnp.swapaxes(from_everyone(first, near), 0, 1)
    return laid_out(pieces.reshape(-1, *array.shape), dim)


def nested_sum(array, axes):
    lines = array.reshape(-1)
    own = sum_in_two_steps(
        padded_to(lines, lax.axis_size(axes[0]) * lax.axis_size(axes[1])), axes, 0
    )
    whole = whole_of(own, axes, 0)
    return whole[: len(lines)].reshape(array.shape)


def taken_together(array, axis):
    return from_everyone(array, axis).sum(axis=0)


def by_axis(array, axes):
    far, near = axes
    return taken_together(taken_together(array, near), far)


def in_one(arrays, axis):
    ravelled, at, outs = (jnp.concatenate([a.reshape(-1) for a in arrays]), 0, [])
    so_far = by_axis(ravelled, axis)
    for a in arrays:
        outs.append(so_far[at : at + a.size].reshape(a.shape))
        at += a.size
    return tuple(outs)


def sweep_rows(gram_block, label_rows, bound_rows, alpha_rows, margin_rows, visit_rows):
    gram_perm = gram_block[visit_rows][:, visit_rows]
    label_perm = label_rows[visit_rows]
    bound_perm = bound_rows[visit_rows]
    alpha_perm = alpha_rows[visit_rows]
    margin_perm = margin_rows[visit_rows]
    diag_perm = jnp.diagonal(gram_perm) + 1e-06

    def update_group(group_index, state_pair):
        alpha_now, margin_now = state_pair
        first_row = jnp.asarray(group_index * GROUP).astype(jnp.int32)
        group_alpha = lax.dynamic_slice_in_dim(alpha_now, first_row, GROUP)
        group_label = lax.dynamic_slice_in_dim(label_perm, first_row, GROUP)
        group_margin = lax.dynamic_slice_in_dim(margin_now, first_row, GROUP)
        group_diag = lax.dynamic_slice_in_dim(diag_perm, first_row, GROUP)
        group_bound = lax.dynamic_slice_in_dim(bound_perm, first_row, GROUP)
        fresh_alpha = jnp.clip(
            group_alpha + (1.0 - group_label * group_margin) / (2.0 * group_diag), 0.0, group_bound
        )
        change = fresh_alpha - group_alpha
        columns = lax.dynamic_slice_in_dim(gram_perm, first_row, GROUP, 1)
        margin_now = margin_now + 2.0 * jnp.dot(
            columns, group_label * change, precision=lax.Precision.HIGHEST
        )
        alpha_now = lax.dynamic_update_slice_in_dim(alpha_now, fresh_alpha, first_row, 0)
        return (alpha_now, margin_now)

    alpha_perm, margin_perm = lax.fori_loop(
        0, alpha_rows.shape[0] // GROUP, update_group, (alpha_perm, margin_perm)
    )
    return jnp.zeros_like(alpha_rows).at[visit_rows].set(alpha_perm)


def body(data_t, labels, sample_weight, w_start, alpha_start, visit_order):
    device_index = lax.axis_index(SHARD)
    devices = lax.axis_size(SHARD)
    local_feat = data_t.shape[0]
    samples = labels.shape[0]
    row_count = alpha_start.shape[0]
    features = local_feat * devices
    label_sign = labels.astype(jnp.float32)
    row_first = device_index * row_count
    own_signs = lax.dynamic_slice_in_dim(label_sign, row_first, row_count)
    own_bound = lax.dynamic_slice_in_dim(sample_weight, row_first, row_count)
    relaid = lax.all_to_all(data_t, SHARD, split_axis=1, concat_axis=0, tiled=True)
    start_part = jnp.dot(w_start.astype(jnp.bfloat16), data_t, preferred_element_type=jnp.float32)
    start_margin = nested_sum(start_part, (("shard_0", "shard_1", "shard_2"), "shard_3"))
    weighted = (
        sample_weight * label_sign * jnp.maximum(0.0, 1.0 - label_sign * start_margin)
    ).astype(jnp.bfloat16)
    ascent = jnp.dot(data_t, weighted, preferred_element_type=jnp.float32)
    column_sq = jnp.einsum("fs,fs->f", data_t, data_t, preferred_element_type=jnp.float32)
    scale_col = column_sq / samples + 1e-06
    stepped = w_start + ascent / (samples * scale_col)
    thresh = 1.0 / (4.0 * features * scale_col)
    primal = stepped - jnp.clip(stepped, -thresh, thresh)
    model_part = jnp.dot(primal.astype(jnp.bfloat16), data_t, preferred_element_type=jnp.float32)
    penalty_part = jnp.sum(jnp.abs(primal)) / (4.0 * features)
    own_margin = sum_in_two_steps(model_part, (("shard_0", "shard_1", "shard_2"), "shard_3"), 0)
    loss_part = jnp.sum(own_bound * jnp.square(jnp.maximum(0.0, 1.0 - own_signs * own_margin))) / (
        2.0 * samples
    )
    loss_total, penalty = in_one(
        (loss_part, penalty_part), (("shard_0", "shard_1", "shard_2"), "shard_3")
    )
    objective = loss_total + penalty
    gram_block = lax.dot_general(
        relaid, relaid, (((0,), (0,)), ((), ())), preferred_element_type=jnp.float32
    )
    block_count = visit_order.shape[0]
    visit_rows = (
        visit_order + (jnp.arange(block_count, dtype=jnp.int32) * visit_order.shape[1])[:, None]
    ).reshape(row_count)
    alpha_zero = own_bound * alpha_start
    alpha_one = sweep_rows(gram_block, own_signs, own_bound, alpha_zero, own_margin, visit_rows)
    change_one = (own_signs * (alpha_one - alpha_zero)).astype(jnp.bfloat16)
    update_part = jnp.dot(relaid, change_one, preferred_element_type=jnp.float32) * (2.0 / devices)
    update_one = by_axis(update_part, (("shard_0", "shard_1"), ("shard_2", "shard_3")))
    second_margin = own_margin + jnp.dot(
        update_one.astype(jnp.bfloat16), relaid, preferred_element_type=jnp.float32
    )
    alpha_two = sweep_rows(gram_block, own_signs, own_bound, alpha_one, second_margin, visit_rows)
    change_two = (own_signs * (alpha_two - alpha_one)).astype(jnp.bfloat16)
    second_part = jnp.dot(relaid, change_two, preferred_element_type=jnp.float32) * (2.0 / devices)
    feat_first = device_index * local_feat
    own_two = sum_in_two_steps(second_part, (("shard_0", "shard_1", "shard_2"), "shard_3"), 0)
    own_one = lax.dynamic_slice_in_dim(update_one, feat_first, local_feat)
    return (primal + own_one + own_two, alpha_two, objective)


def solution(mesh):
    torus = Mesh(mesh.devices.reshape(4, 4, 4, 2), ("shard_0", "shard_1", "shard_2", "shard_3"))
    in_specs = (P(SHARD, None), P(), P(), P(SHARD), P(SHARD), P(SHARD, None))
    out_specs = (P(SHARD), P(SHARD), P())
    return jax.shard_map(body, mesh=torus, in_specs=in_specs, out_specs=out_specs, check_vma=False)
```

profile of v0, /device:TPU:1, one launch (start us, length us, event | category | flops | bytes accessed | tf_op | source)
XLA Modules:
  0.0 239.2 jit_solution(1073073337814106719)
XLA Ops:
  3.6 5.0 %all_to_all.96 = f32[2,64,256]{2,1,0:T(8,128)S(1)} all-to-all(f32[2,64,256]{2,1,0:T(8,128)S(1)} %copy.41), channel_id=1, replica_groups=mesh['shard_0'=4,'shard_1'=4,'shard_2'=4,'shard_3'=2] {'shard_3'}, dimensions={0} | all-to-all | bytes 262144 | tf_op jit(solution)/shard_map/all_to_all | solution.py:18
  8.7 19.6 %all_to_all.97 = f32[64,1,256]{2,1,0:T(1,128)S(1)} all-to-all(f32[64,1,256]{2,1,0:T(1,128)S(1)} %all_to_all.65), channel_id=1, replica_groups=mesh['shard_0'=4,'shard_1'=4,'shard_2'=4,'shard_3'=2] {'shard_0','shard_..., dimensions={0} | all-to-all | bytes 131072 | tf_op jit(solution)/shard_map/all_to_all | solution.py:25
  29.1 5.0 %all-to-all-start.2 = ((f32[64,1,256]{2,1,0:T(1,128)}), f32[64,1,256]{2,1,0:T(1,128)S(1)}, u32[]{:S(2)}, u32[]{:S(2)}) async-start(f32[64,1,256]{2,1,0:T(1,128)} %broadcast_in_dim.18), calls=%async_computation.2 | async-start | bytes 131072 | tf_op jit(solution)/shard_map/all_to_all | solution.py:37
  37.1 5.3 %all-to-all-done.2 = f32[64,1,256]{2,1,0:T(1,128)S(1)} async-done(((f32[64,1,256]{2,1,0:T(1,128)}), f32[64,1,256]{2,1,0:T(1,128)S(1)}, u32[]{:S(2)}, u32[]{:S(2)}) %all-to-all-start.2) | async-done | bytes 65568 | tf_op jit(solution)/shard_map/all_to_all | solution.py:37
  42.5 6.7 %all_to_all.98 = f32[2,64,256]{2,1,0:T(8,128)S(1)} all-to-all(f32[2,64,256]{2,1,0:T(8,128)S(1)} %broadcast_in_dim.20), channel_id=1, replica_groups=mesh['shard_0'=4,'shard_1'=4,'shard_2'=4,'shard_3'=2] {'shard_3'}, dimensions={0} | all-to-all | bytes 262144 | tf_op jit(solution)/shard_map/all_to_all | solution.py:37
  49.5 4.0 %abs_reduce_fusion = (f32[]{:T(128)}, f32[64]{0:T(128)S(1)}, f32[64]{0:T(128)S(1)}) fusion(f32[64]{0:T(128)S(1)} %fusion.16, f32[64]{0:T(128)S(1)} %copy-done.6, bf16[32768,1]{0,1:T(2,128)(2,1)S(1)} %reshape.186, bf16[64,32768]{1,0:T(8,128)(2,1)} %param.10), kind=kOutput, calls=%fused_computation.56 | convolution fusion | flops 4195071 | bytes 4260868 | tf_op jit(solution)/shard_map/dot_general | solution.py:132
  54.3 3.8 %all_to_all.99 = f32[2,64,256]{2,1,0:T(8,128)S(1)} all-to-all(f32[2,64,256]{2,1,0:T(8,128)S(1)} %copy.43), channel_id=1, replica_groups=mesh['shard_0'=4,'shard_1'=4,'shard_2'=4,'shard_3'=2] {'shard_3'}, dimensions={0} | all-to-all | bytes 262144 | tf_op jit(solution)/shard_map/all_to_all | solution.py:18
  58.8 4.7 %all-to-all-start.5 = ((f32[64,1,256]{2,1,0:T(1,128)}), f32[64,1,256]{2,1,0:T(1,128)S(1)}, u32[]{:S(2)}, u32[]{:S(2)}) async-start(f32[64,1,256]{2,1,0:T(1,128)} %all_to_all.70), calls=%async_computation.5 | async-start | bytes 131072 | tf_op jit(solution)/shard_map/all_to_all | solution.py:25
  63.5 4.7 %copy.68 = bf16[8,128,8,256]{3,2,0,1:T(8,128)(2,1)} copy(bf16[8,128,8,256]{3,2,1,0:T(8,128)(2,1)} %bitcast.76) | data formatting | bytes 8388608 | tf_op jit(solution)/shard_map/all_to_all | solution.py:126
  68.2 3.7 %all-to-all-done.5 = f32[64,1,256]{2,1,0:T(1,128)S(1)} async-done(((f32[64,1,256]{2,1,0:T(1,128)}), f32[64,1,256]{2,1,0:T(1,128)S(1)}, u32[]{:S(2)}, u32[]{:S(2)}) %all-to-all-start.5) | async-done | bytes 65568 | tf_op jit(solution)/shard_map/all_to_all | solution.py:25
  71.9 6.5 %all-to-all-start.6 = ((bf16[64,128,256]{2,0,1:T(8,128)(2,1)}), bf16[64,128,256]{2,0,1:T(8,128)(2,1)}, u32[]{:S(2)}, u32[]{:S(2)}) async-start(bf16[64,128,256]{2,0,1:T(8,128)(2,1)} %bitcast.77), calls=%async_computation.6 | async-start | bytes 8388608 | tf_op jit(solution)/shard_map/all_to_all | solution.py:126
  88.5 42.7 %all-to-all-done.6 = bf16[64,128,256]{2,0,1:T(8,128)(2,1)} async-done(((bf16[64,128,256]{2,0,1:T(8,128)(2,1)}), bf16[64,128,256]{2,0,1:T(8,128)(2,1)}, u32[]{:S(2)}, u32[]{:S(2)}) %all-to-all-start.6) | async-done | bytes 4194336 | tf_op jit(solution)/shard_map/all_to_all | solution.py:126
  131.8 4.1 %all-to-all-start.11 = ((f32[2,1,2]{2,1,0:T(1,128)}), f32[2,1,2]{2,1,0:T(1,128)S(1)}, u32[]{:S(2)}, u32[]{:S(2)}) async-start(f32[2,1,2]{2,1,0:T(1,128)} %broadcast_in_dim.23), calls=%async_computation.11 | async-start | bytes 2048 | tf_op jit(solution)/shard_map/all_to_all | solution.py:37
  135.9 4.7 %fusion.19 = f32[256,256]{1,0:T(8,128)S(1)} fusion(bf16[64,128,256]{2,0,1:T(8,128)(2,1)} %all-to-all-done.6), kind=kOutput, calls=%fused_computation.36 | convolution fusion | flops 1073741824 | bytes 4456448 | tf_op jit(solution)/shard_map/dot_general | solution.py:148
  145.3 8.5 %while.30 = (s32[]{:T(128)}, f32[256]{0:T(256)S(1)}, f32[256]{0:T(256)S(1)}, f32[256]{0:T(256)S(1)}, f32[256]{0:T(256)S(1)}, /*index=5*/f32[256]{0:T(256)S(1)}, ...) while((s32[]{:T(128)}, f32[256]{0:T(256)S(1)}, f32[256]{0:T(256)S(1)}, ...), condition=%wide.region_5.6_spmd, body=%wide.region_4.5_spmd.sunk | while | flops 49814 | bytes 145567 | solution.py:109
  162.9 6.5 %all-to-all-done.7 = f32[8,1,8192]{2,1,0:T(1,128)S(1)} async-done(((f32[8,1,8192]{2,1,0:T(1,128)}), f32[8,1,8192]{2,1,0:T(1,128)S(1)}, u32[]{:S(2)}, u32[]{:S(2)}) %all-to-all-start.7) | async-done | bytes 262176 | tf_op jit(solution)/shard_map/all_to_all | solution.py:37
  170.0 4.5 %all-to-all-start.12 = ((f32[64,1,2]{2,1,0:T(1,128)}), f32[64,1,2]{2,1,0:T(1,128)S(1)}, u32[]{:S(2)}, u32[]{:S(2)}) async-start(f32[64,1,2]{2,1,0:T(1,128)} %broadcast_in_dim.24), calls=%async_computation.12 | async-start | bytes 65536 | tf_op jit(solution)/shard_map/all_to_all | solution.py:37
  174.8 8.2 %all-to-all-done.12 = f32[64,1,2]{2,1,0:T(1,128)S(1)} async-done(((f32[64,1,2]{2,1,0:T(1,128)}), f32[64,1,2]{2,1,0:T(1,128)S(1)}, u32[]{:S(2)}, u32[]{:S(2)}) %all-to-all-start.12) | async-done | bytes 544 | tf_op jit(solution)/shard_map/all_to_all | solution.py:37
  184.2 3.6 %all-to-all-start.8 = ((f32[16,1,8192]{2,1,0:T(1,128)}), f32[16,1,8192]{2,1,0:T(1,128)S(1)}, u32[]{:S(2)}, u32[]{:S(2)}) async-start(f32[16,1,8192]{2,1,0:T(1,128)} %broadcast_in_dim.22), calls=%async_computation.8 | async-start | bytes 1048576 | tf_op jit(solution)/shard_map/all_to_all | solution.py:37
  189.8 7.4 %all-to-all-done.8 = f32[16,1,8192]{2,1,0:T(1,128)S(1)} async-done(((f32[16,1,8192]{2,1,0:T(1,128)}), f32[16,1,8192]{2,1,0:T(1,128)S(1)}, u32[]{:S(2)}, u32[]{:S(2)}) %all-to-all-start.8) | async-done | bytes 524320 | tf_op jit(solution)/shard_map/all_to_all | solution.py:37
  202.4 8.5 %while.31 = (s32[]{:T(128)}, f32[256]{0:T(256)S(1)}, f32[256]{0:T(256)S(1)}, f32[256]{0:T(256)S(1)}, f32[256]{0:T(256)S(1)}, /*index=5*/f32[256]{0:T(256)S(1)}, ...) while((s32[]{:T(128)}, f32[256]{0:T(256)S(1)}, f32[256]{0:T(256)S(1)}, ...), condition=%wide.region_10.11_spmd, body=%wide.region_9.10_spmd.sunk | while | flops 49814 | bytes 145567 | solution.py:109
  215.9 6.5 %all_to_all.100 = f32[2,1,4096]{2,1,0:T(1,128)S(1)} all-to-all(f32[2,1,4096]{2,1,0:T(1,128)S(1)} %reshape.203), channel_id=1, replica_groups=mesh['shard_0'=4,'shard_1'=4,'shard_2'=4,'shard_3'=2] {'shard_3'}, dimensions={0} | all-to-all | bytes 65536 | tf_op jit(solution)/shard_map/all_to_all | solution.py:18
  224.3 4.6 %all-to-all-start.10 = ((f32[64,1,64]{2,1,0:T(1,128)}), f32[64,1,64]{2,1,0:T(1,128)S(1)}, u32[]{:S(2)}, u32[]{:S(2)}) async-start(f32[64,1,64]{2,1,0:T(1,128)} %bitcast.24), calls=%async_computation.10 | async-start | bytes 65536 | tf_op jit(solution)/shard_map/all_to_all | solution.py:25
  230.9 6.5 %all-to-all-done.10 = f32[64,1,64]{2,1,0:T(1,128)S(1)} async-done(((f32[64,1,64]{2,1,0:T(1,128)}), f32[64,1,64]{2,1,0:T(1,128)S(1)}, u32[]{:S(2)}, u32[]{:S(2)}) %all-to-all-start.10) | async-done | bytes 16416 | tf_op jit(solution)/shard_map/all_to_all | solution.py:25
  (249 shorter events, 64.6 us)
Async XLA Ops:
  3.5 45.9 %copy-start.1 = (s32[32768]{0:T(1024)S(1)}, s32[32768]{0:T(1024)}, u32[]{:S(2)}) copy-start(s32[32768]{0:T(1024)} %param.11) | copy-start | bytes 393220
  3.5 45.9 %copy-start.2 = (f32[32768]{0:T(1024)S(1)}, f32[32768]{0:T(1024)}, u32[]{:S(2)}) copy-start(f32[32768]{0:T(1024)} %param.12) | copy-start | bytes 393220
  3.5 46.0 %copy-start.6 = (f32[64]{0:T(128)S(1)}, f32[64]{0:T(128)}, u32[]{:S(2)}) copy-start(f32[64]{0:T(128)} %param.13) | copy-start | bytes 772
  29.1 13.4 %all-to-all-start.2 = ((f32[64,1,256]{2,1,0:T(1,128)}), f32[64,1,256]{2,1,0:T(1,128)S(1)}, u32[]{:S(2)}, u32[]{:S(2)}) async-start(f32[64,1,256]{2,1,0:T(1,128)} %broadcast_in_dim.18), calls=%async_computation.2 | async-start | bytes 131072 | tf_op jit(solution)/shard_map/all_to_all | solution.py:37
  42.5 11.0 %copy-start = (bf16[64,32768]{1,0:T(8,128)(2,1)S(1)}, bf16[64,32768]{1,0:T(8,128)(2,1)}, u32[]{:S(2)}) copy-start(bf16[64,32768]{1,0:T(8,128)(2,1)} %param.10) | copy-start | bytes 12582916
  58.8 13.1 %all-to-all-start.5 = ((f32[64,1,256]{2,1,0:T(1,128)}), f32[64,1,256]{2,1,0:T(1,128)S(1)}, u32[]{:S(2)}, u32[]{:S(2)}) async-start(f32[64,1,256]{2,1,0:T(1,128)} %all_to_all.70), calls=%async_computation.5 | async-start | bytes 131072 | tf_op jit(solution)/shard_map/all_to_all | solution.py:25
  71.9 6.5 %copy-start.5 = (s32[2,128]{1,0:T(2,128)S(1)}, s32[2,128]{1,0:T(2,128)}, u32[]{:S(2)}) copy-start(s32[2,128]{1,0:T(2,128)} %param.15) | copy-start | bytes 3076
  71.9 13.9 %copy-start.3 = (f32[256]{0:T(256)S(1)}, f32[256]{0:T(256)}, u32[]{:S(2)}) copy-start(f32[256]{0:T(256)} %param.14) | copy-start | bytes 3076
  71.9 59.3 %all-to-all-start.6 = ((bf16[64,128,256]{2,0,1:T(8,128)(2,1)}), bf16[64,128,256]{2,0,1:T(8,128)(2,1)}, u32[]{:S(2)}, u32[]{:S(2)}) async-start(bf16[64,128,256]{2,0,1:T(8,128)(2,1)} %bitcast.77), calls=%async_computation.6 | async-start | bytes 8388608 | tf_op jit(solution)/shard_map/all_to_all | solution.py:126
  131.8 26.8 %all-to-all-start.11 = ((f32[2,1,2]{2,1,0:T(1,128)}), f32[2,1,2]{2,1,0:T(1,128)S(1)}, u32[]{:S(2)}, u32[]{:S(2)}) async-start(f32[2,1,2]{2,1,0:T(1,128)} %broadcast_in_dim.23), calls=%async_computation.11 | async-start | bytes 2048 | tf_op jit(solution)/shard_map/all_to_all | solution.py:37
  159.4 10.0 %all-to-all-start.7 = ((f32[8,1,8192]{2,1,0:T(1,128)}), f32[8,1,8192]{2,1,0:T(1,128)S(1)}, u32[]{:S(2)}, u32[]{:S(2)}) async-start(f32[8,1,8192]{2,1,0:T(1,128)} %broadcast_in_dim.21), calls=%async_computation.7 | async-start | bytes 524288 | tf_op jit(solution)/shard_map/all_to_all | solution.py:37
  170.0 13.0 %all-to-all-start.12 = ((f32[64,1,2]{2,1,0:T(1,128)}), f32[64,1,2]{2,1,0:T(1,128)S(1)}, u32[]{:S(2)}, u32[]{:S(2)}) async-start(f32[64,1,2]{2,1,0:T(1,128)} %broadcast_in_dim.24), calls=%async_computation.12 | async-start | bytes 65536 | tf_op jit(solution)/shard_map/all_to_all | solution.py:37
  184.2 13.0 %all-to-all-start.8 = ((f32[16,1,8192]{2,1,0:T(1,128)}), f32[16,1,8192]{2,1,0:T(1,128)S(1)}, u32[]{:S(2)}, u32[]{:S(2)}) async-start(f32[16,1,8192]{2,1,0:T(1,128)} %broadcast_in_dim.22), calls=%async_computation.8 | async-start | bytes 1048576 | tf_op jit(solution)/shard_map/all_to_all | solution.py:37
  212.3 25.8 %copy-start.4 = (f32[256]{0:T(256)}, f32[256]{0:T(256)S(1)}, u32[]{:S(2)}) copy-start(f32[256]{0:T(256)S(1)} %scatter_custom_fusion.1) | copy-start | bytes 3076
  224.3 13.1 %all-to-all-start.10 = ((f32[64,1,64]{2,1,0:T(1,128)}), f32[64,1,64]{2,1,0:T(1,128)S(1)}, u32[]{:S(2)}, u32[]{:S(2)}) async-start(f32[64,1,64]{2,1,0:T(1,128)} %bitcast.24), calls=%async_computation.10 | async-start | bytes 65536 | tf_op jit(solution)/shard_map/all_to_all | solution.py:25
where the time goes:
time: 240 us; the launch traced here: 239 us
  waiting for transfers between devices  80.4 us (34%)
  blocking collectives  41.6 us (17%)
  starting transfers between devices  36.5 us (15%)
  local copies, waits for them, and re-layouts  30.4 us (13%)
  matrix products  29.8 us (12%)
  other arithmetic  14.3 us (6%)
  between operations  4.83 us (2%)
    all_to_all x1, waiting for transfers between devices, body(): lax.all_to_all(data_t, SHARD, split_axis=1, concat_axis=0, tiled=True)  42.7 us
    all_to_all x5, waiting for transfers between devices, from_everyone(): lax.all_to_all(jnp.broadcast_to(array[None], (size, *array.shape)), axis,...  27.4 us
    all_to_all x5, starting transfers between devices, from_everyone(): lax.all_to_all(jnp.broadcast_to(array[None], (size, *array.shape)), axis,...  20.7 us
    all_to_all x1, blocking collectives, sum_in_two_steps(): return jnp.sum(lax.all_to_all(own, far, 0, 0, tiled=True), axis=0)  19.6 us
    all_to_all x3, blocking collectives, sum_at_owner(): pieces = lax.all_to_all(cut_along(array, dim, size), axis, 0, 0, tiled=True)  15.3 us
    all_to_all x2, waiting for transfers between devices, sum_in_two_steps(): return jnp.sum(lax.all_to_all(own, far, 0, 0, tiled=True), axis=0)  10.2 us
    all_to_all x2, starting transfers between devices, sum_in_two_steps(): return jnp.sum(lax.all_to_all(own, far, 0, 0, tiled=True), axis=0)  9.3 us
    dot_general x32, matrix products, update_group(): jnp.dot(columns, group_label * change, precision=lax.Precision.HIGHEST)  7.97 us
  transfers between devices with their start and end apart: 8, of which 7 were waited for; matrix products, arithmetic and copies ran while one was open for 17% of the time, Pallas kernels for 0%

commit v1 on v0

v1 whole, which is shorter than its diff:
```python
import functools

import jax
import jax.numpy as jnp
from jax import lax
from jax.experimental import pallas as pl
from jax.experimental.pallas import tpu as pltpu
from jax.sharding import PartitionSpec as P

F32 = jnp.float32
BF16 = jnp.bfloat16
MESH = pl.DeviceIdType.MESH
AXIS = "shard"
GROUP = 16
BATCHES = 4


def kernel(devices, samples, x_hbm, lab_hbm, wgt_hbm, w_ref, start_ref, visit_ref,
           weights_ref, alpha_ref, objective_ref,
           x, raw, own_lab, own_wgt, send, recv, h_all, z_all, obj_all,
           gram, perm, onehot, onehot_t, mc, yc, cc, ac, ic, zc, zown,
           load_sem, small_sem, own_sem, bulk_send, bulk_recv,
           rs_send, rs_recv, ag_send, ag_recv, obj_send, obj_recv):
    me = lax.axis_index(AXIS)
    local = x.shape[0]
    features = local * devices
    rows = 256
    others = devices - 1

    def target(k):
        o = lax.rem(k * 37, devices)
        c = lax.rem(me + o, 2)
        y = lax.rem(me // 2 + o // 2, 4)
        xx = lax.rem(me // 8 + o // 8, 4)
        z = lax.rem(me // 32 + o // 32, 4)
        return ((z * 4 + xx) * 4 + y) * 2 + c

    barrier = pltpu.get_barrier_semaphore()

    def greet(k, carry):
        pl.semaphore_signal(barrier, inc=1, device_id=(target(k),), device_id_type=MESH)
        return carry

    lax.fori_loop(1, devices, greet, 0)

    pieces = load_sem.shape[0]
    width = samples // pieces

    def load(i):
        at = pl.ds(i * width, width)
        return pltpu.make_async_copy(x_hbm.at[:, at], x.at[:, at], load_sem.at[i])

    for i in range(pieces):
        load(i).start()
    lab_copy = pltpu.make_async_copy(lab_hbm.at[me], own_lab, small_sem.at[0])
    wgt_copy = pltpu.make_async_copy(wgt_hbm.at[me], own_wgt, small_sem.at[1])
    lab_copy.start()
    wgt_copy.start()
    own_copy = pltpu.make_async_copy(
        x_hbm.at[:, pl.ds(pl.multiple_of(me * rows, rows), rows)], raw.at[others], own_sem
    )
    own_copy.start()

    eye = lax.broadcasted_iota(jnp.int32, (local, local), 0) == lax.broadcasted_iota(
        jnp.int32, (local, local), 1
    )

    def to_row(col):
        return jnp.sum(jnp.where(eye, col, 0.0), axis=0, keepdims=True)

    def to_col(row):
        return jnp.sum(jnp.where(eye, row, 0.0), axis=1, keepdims=True)

    chunk = 2048

    def margins(row, phase, first, last):
        lhs = jnp.broadcast_to(row, (8, local)).astype(BF16)

        def one(i, carry):
            out = jnp.dot(
                lhs, x[:, pl.ds(pl.multiple_of(i * chunk, chunk), chunk)],
                preferred_element_type=F32,
            )
            for j in range(chunk // 128):
                send[phase, i * (chunk // rows) + j // 2, j % 2 : j % 2 + 1, :] = out[
                    0:1, 128 * j : 128 * j + 128
                ]
            return carry

        lax.fori_loop(first, last, one, 0)

    def scatter(phase):
        def one(k, carry):
            to = target(k)
            pltpu.make_async_remote_copy(
                src_ref=send.at[phase, to], dst_ref=recv.at[phase, me],
                send_sem=rs_send.at[phase], recv_sem=rs_recv.at[phase],
                device_id=(to,), device_id_type=MESH,
            ).start()
            return carry

        recv[phase, me] = send[phase, me]
        lax.fori_loop(1, devices, one, 0)

    def scattered(phase):
        many = recv.at[phase, pl.ds(0, others)]
        pltpu.make_async_copy(many, many, rs_recv.at[phase]).wait()
        return jnp.sum(recv[phase], axis=0)

    def gather(src, buf, send_sem, recv_sem):
        def one(k, carry):
            pltpu.make_async_remote_copy(
                src_ref=src, dst_ref=buf.at[me],
                send_sem=send_sem, recv_sem=recv_sem,
                device_id=(target(k),), device_id_type=MESH,
            ).start()
            return carry

        lax.fori_loop(1, devices, one, 0)

    def drain(buf, sem):
        many = buf.at[pl.ds(0, others)]
        pltpu.make_async_copy(many, many, sem).wait()

    def bulk(batch):
        def one(k, carry):
            to = target(k)
            pltpu.make_async_remote_copy(
                src_ref=x.at[:, pl.ds(pl.multiple_of(to * rows, rows), rows)],
                dst_ref=raw.at[k - 1],
                send_sem=bulk_send.at[batch], recv_sem=bulk_recv.at[batch],
                device_id=(to,), device_id_type=MESH,
            ).start()
            return carry

        size = devices // BATCHES
        lax.fori_loop(batch * size + 1, min((batch + 1) * size, others) + 1, one, 0)

    def batch_slots(batch):
        size = devices // BATCHES
        return raw.at[pl.ds(batch * size, min((batch + 1) * size, others) - batch * size)]

    def contract(buf):
        def one(d, acc):
            part = x[:, pl.ds(pl.multiple_of(d * rows, rows), rows)].astype(F32)
            v = buf[d].astype(F32)
            return acc + part[:, :128] * v[0:1] + part[:, 128:] * v[1:2]

        acc = lax.fori_loop(0, devices, one, jnp.zeros((local, 128), F32), unroll=4)
        return jnp.sum(acc, axis=1, keepdims=True)

    w_row = w_ref[...]
    per = width // chunk
    for i in range(pieces):
        load(i).wait()
        margins(w_row, 0, i * per, (i + 1) * per)
    pl.semaphore_wait(barrier, others)
    scatter(0)
    bulk(0)

    def square(d, acc):
        part = x[:, pl.ds(pl.multiple_of(d * rows, rows), rows)].astype(F32)
        return acc + part[:, :128] * part[:, :128] + part[:, 128:] * part[:, 128:]

    sq = lax.fori_loop(0, devices, square, jnp.zeros((local, 128), F32), unroll=4)
    scale = jnp.sum(sq, axis=1, keepdims=True) / samples + 1e-06
    lab_copy.wait()
    wgt_copy.wait()
    sign = own_lab[...].astype(F32)
    bound = own_wgt[...]

    v0 = scattered(0)
    h_all[me] = (bound * sign * jnp.maximum(0.0, 1.0 - sign * v0)).astype(BF16)
    gather(h_all.at[me], h_all, ag_send.at[0], ag_recv.at[0])
    bulk(1)
    alpha0 = bound * start_ref[...]
    lane = lax.broadcasted_iota(jnp.int32, (128, 128), 1)
    sub = lax.broadcasted_iota(jnp.int32, (128, 128), 0)

    def permuted(vec, b):
        col = jnp.sum(onehot[b] * vec[b : b + 1], axis=1, keepdims=True)
        return jnp.broadcast_to(col, (128, 128))

    for b in range(2):
        hot = jnp.where(sub == visit_ref[b : b + 1, :], 1.0, 0.0)
        onehot_t[b] = hot.astype(BF16)
        onehot[b] = jnp.transpose(hot)
    for b in range(2):
        part = slice(128 * b, 128 * b + 128)
        yc[part] = permuted(sign, b)
        cc[part] = permuted(bound, b)
        ac[part] = permuted(alpha0, b)

    drain(h_all, ag_recv.at[0])
    w_col = to_col(w_row)
    stepped = w_col + contract(h_all) / (samples * scale)
    thresh = 1.0 / (4.0 * features * scale)
    primal = stepped - jnp.clip(stepped, -thresh, thresh)
    penalty = jnp.sum(jnp.abs(primal)) / (4.0 * features)
    margins(to_row(primal), 1, 0, samples // chunk)
    scatter(1)
    for batch in range(2, BATCHES):
        bulk(batch)
    v1 = scattered(1)
    loss = jnp.sum(bound * jnp.square(jnp.maximum(0.0, 1.0 - sign * v1))) / (2.0 * samples)
    obj_all[me] = jnp.full((1, 128), loss + penalty, F32)

    own_copy.wait()
    gram[...] = jnp.zeros_like(gram)
    size = devices // BATCHES
    for batch in range(BATCHES):
        slots = batch_slots(batch)
        pltpu.make_async_copy(slots, slots, bulk_recv.at[batch]).wait()

        def one(i, carry):
            piece = raw[pl.ds(batch * size + i * 16, 16)].reshape(16 * local, rows)
            gram[...] += lax.dot_general(
                piece, piece, (((0,), (0,)), ((), ())), preferred_element_type=F32
            )
            return carry

        lax.fori_loop(0, size // 16, one, 0)

    def halves(a):
        hi = a.astype(BF16)
        return hi, (a - hi.astype(F32)).astype(BF16)

    for b in range(2):
        cols = slice(128 * b, 128 * b + 128)
        hi, lo = halves(gram[:, cols])
        perm[:, cols] = jnp.dot(hi, onehot_t[b], preferred_element_type=F32) + jnp.dot(
            lo, onehot_t[b], preferred_element_type=F32
        )
    for b in range(2):
        part = slice(128 * b, 128 * b + 128)
        left = onehot[b].astype(BF16)
        hi, lo = halves(perm[part, :])
        gram[part, :] = jnp.dot(left, hi, preferred_element_type=F32) + jnp.dot(
            left, lo, preferred_element_type=F32
        )
    for b in range(2):
        part = slice(128 * b, 128 * b + 128)
        diag = jnp.sum(jnp.where(lane == sub, gram[part, part], 0.0), axis=1, keepdims=True)
        ic[part] = jnp.broadcast_to(1.0 / (2.0 * (diag + 1e-06)), (128, 128))

    lane16 = lax.broadcasted_iota(jnp.int32, (GROUP, 128), 1)
    sub16 = lax.broadcasted_iota(jnp.int32, (GROUP, 128), 0)

    def sweep(margin):
        for b in range(2):
            mc[128 * b : 128 * b + 128] = permuted(margin, b)
        c = [jnp.zeros((1, 128), F32), jnp.zeros((1, 128), F32)]
        for t in range(rows // GROUP):
            at = slice(GROUP * t, GROUP * t + GROUP)
            b, first = t // 8, GROUP * (t % 8)
            prod = gram[at, 0:128] * c[0]
            if b:
                prod = prod + gram[at, 128:256] * c[1]
            m = mc[at] + 2.0 * jnp.sum(prod, axis=1, keepdims=True)
            old, y = ac[at], yc[at]
            new = jnp.clip(old + (1.0 - y * m) * ic[at], 0.0, cc[at])
            step = y * (new - old)
            ac[at] = new
            zc[at] = step
            c[b] = c[b] + jnp.sum(
                jnp.where(lane16 == sub16 + first, step, 0.0), axis=0, keepdims=True
            )

    def natural(col, b):
        return jnp.sum(onehot[b] * col[128 * b : 128 * b + 128], axis=0, keepdims=True)

    sweep(v1)
    for b in range(2):
        zown[b : b + 1] = natural(zc, b)
    z_all[0, me] = zown[...].astype(BF16)
    gather(z_all.at[0, me], z_all.at[0], ag_send.at[1], ag_recv.at[1])
    gather(obj_all.at[me], obj_all, obj_send, obj_recv)
    drain(z_all.at[0], ag_recv.at[1])
    first_dw = contract(z_all.at[0]) * (2.0 / devices)
    margins(to_row(first_dw), 2, 0, samples // chunk)
    scatter(2)
    v2 = v1 + scattered(2)
    sweep(v2)
    for b in range(2):
        zown[b : b + 1] = natural(zc, b)
    z_all[1, me] = zown[...].astype(BF16)
    gather(z_all.at[1, me], z_all.at[1], ag_send.at[2], ag_recv.at[2])
    for b in range(2):
        alpha_ref[b : b + 1] = natural(ac, b)
    drain(obj_all, obj_recv)
    objective_ref[...] = jnp.sum(obj_all[...], axis=0)
    for phase in range(3):
        drain(send.at[phase], rs_send.at[phase])
    drain(h_all, ag_send.at[0])
    drain(z_all.at[0], ag_send.at[1])
    drain(obj_all, obj_send)
    for batch in range(BATCHES):
        slots = batch_slots(batch)
        pltpu.make_async_copy(slots, slots, bulk_send.at[batch]).wait()
    drain(z_all.at[1], ag_recv.at[2])
    second_dw = contract(z_all.at[1]) * (2.0 / devices)
    weights_ref[...] = to_row(primal + first_dw + second_dw)
    drain(z_all.at[1], ag_send.at[2])


def solution(mesh):
    devices = mesh.shape[AXIS]

    def body(data_t, labels, sample_weight, w_start, alpha_start, visit_order):
        local, samples = data_t.shape
        per = samples // devices
        anyspace = pl.BlockSpec(memory_space=pl.ANY)
        vmem = pl.BlockSpec(memory_space=pltpu.VMEM)
        square = pltpu.VMEM((per, 128), F32)
        dma = pltpu.SemaphoreType.DMA
        weights, alpha, objective = pl.pallas_call(
            functools.partial(kernel, devices, samples),
            out_shape=(
                jax.ShapeDtypeStruct((1, local), F32),
                jax.ShapeDtypeStruct((2, 128), F32),
                jax.ShapeDtypeStruct((1, 128), F32),
            ),
            in_specs=[anyspace, anyspace, anyspace, vmem, vmem, vmem],
            out_specs=(vmem, vmem, vmem),
            scratch_shapes=[
                pltpu.VMEM((local, samples), BF16),
                pltpu.VMEM((devices, local, per), BF16),
                pltpu.VMEM((2, 128), jnp.int32),
                pltpu.VMEM((2, 128), F32),
                pltpu.VMEM((3, devices, 2, 128), F32),
                pltpu.VMEM((3, devices, 2, 128), F32),
                pltpu.VMEM((devices, 2, 128), BF16),
                pltpu.VMEM((2, devices, 2, 128), BF16),
                pltpu.VMEM((devices, 1, 128), F32),
                pltpu.VMEM((per, per), F32),
                pltpu.VMEM((per, per), F32),
                pltpu.VMEM((2, 128, 128), F32),
                pltpu.VMEM((2, 128, 128), BF16),
                square, square, square, square, square, square,
                pltpu.VMEM((2, 128), F32),
                dma((8,)), dma((2,)), dma, dma((BATCHES,)), dma((BATCHES,)),
                dma((3,)), dma((3,)), dma((3,)), dma((3,)), dma, dma,
            ],
            compiler_params=pltpu.CompilerParams(collective_id=0, has_side_effects=True),
        )(
            data_t,
            labels.reshape(devices, 2, 128),
            sample_weight.reshape(devices, 2, 128),
            w_start.reshape(1, local),
            alpha_start.reshape(2, 128),
            visit_order,
        )
        return weights.reshape(local), alpha.reshape(per), objective[0, 0]

    return jax.shard_map(
        body,
        mesh=mesh,
        in_specs=(P(AXIS, None), P(), P(), P(AXIS), P(AXIS), P(AXIS, None)),
        out_specs=(P(AXIS), P(AXIS), P()),
        check_vma=False,
    )
```

time: 240 us -> 123 us (0.51)
  Pallas kernels: 0 us -> 118 us
  waiting for transfers between devices: 80.4 us -> 0 us
  blocking collectives: 41.6 us -> 0 us
  starting transfers between devices: 36.5 us -> 0 us
  matrix products: 29.8 us -> 0 us
  local copies, waits for them, and re-layouts: 30.4 us -> 2.36 us
  other arithmetic: 14.3 us -> 0 us
  between operations: 4.83 us -> 2.4 us
    pallas_call x0 -> x1, Pallas kernels: none -> 118 us  [body(): pl.pallas_call(functools.partial(kernel, devices, samples), out_shape=(ja...]
    all_to_all x8 -> x0, waiting for transfers between devices: 80.4 us -> none  [the longest x1 42.7 us: body(): lax.all_to_all(data_t, SHARD, split_axis=1, concat_axis=0, tiled=True)]
    all_to_all x5 -> x0, blocking collectives: 41.6 us -> none  [the longest x1 19.6 us: sum_in_two_steps(): return jnp.sum(lax.all_to_all(own, far, 0, 0, tiled=True), axis=0)]
    all_to_all x8 -> x0, starting transfers between devices: 36.5 us -> none  [the longest x5 20.7 us: from_everyone(): lax.all_to_all(jnp.broadcast_to(array[None], (size, *array.shape)), axis,...]
    dot_general x39 -> x0, matrix products: 29.8 us -> none  [the longest x32 7.97 us: update_group(): jnp.dot(columns, group_label * change, precision=lax.Precision.HIGHEST)]
    gather x10 -> x0, local copies, waits for them, and re-layouts: 16.1 us -> none  [the longest x2 3.89 us: sweep_rows(): margin_perm = margin_rows[visit_rows]]
    all_to_all x4 -> x0, local copies, waits for them, and re-layouts: 5.97 us -> none  [the longest x1 4.74 us: body(): lax.all_to_all(data_t, SHARD, split_axis=1, concat_axis=0, tiled=True)]
    dynamic_update_slice x32 -> x0, other arithmetic: 5.71 us -> none  [update_group(): lax.dynamic_update_slice_in_dim(alpha_now, fresh_alpha, first_row, 0)]
  transfers between devices with their start and end apart: 8 -> 0, of which waited for: 7 -> 0; matrix products, arithmetic and copies ran while one was open for 17% -> 0% of each run, Pallas kernels for 0% -> 0%
where the time goes in v1:
time: 123 us; the launch traced here: 122 us
  Pallas kernels  118 us (96%)
  between operations  2.4 us (2%)
  local copies, waits for them, and re-layouts  2.36 us (2%)
    pallas_call x1, Pallas kernels, body(): pl.pallas_call(functools.partial(kernel, devices, samples), out_shape=(ja...  118 us

profile of v1, /device:TPU:1, one launch (start us, length us, event | category | flops | bytes accessed | tf_op | source)
XLA Modules:
  0.0 122.4 jit_solution(12061434451676955458)
XLA Ops:
  0.6 117.6 %shard_map.85 = (f32[1,64]{1,0:T(1,128)}, f32[2,128]{1,0:T(2,128)}, f32[1,128]{1,0:T(1,128)}) custom-call(bf16[64,32768]{1,0:T(8,128)(2,1)} %x_hbm.1, s32[128,2,128]{2,1,0:T(2,128)} %bitcast.8, f32[128,2,128]{2,1,0:T(2,128)} %bitcast.9, f32[1,64]{1,0:T(1,128)} %bitcast.12, f32[2,128]{1,0:T(2,128)} %bitcast.10, s32[2,128]{1,0:T(2,128)} %visit_ref.1), custom_call_target="tpu_custom_call" | custom-call | tf_op jit(solution)/shard_map/pallas_call | solution.py:316
  118.3 1.1 copy.12
  119.4 1.2 copy.13

commit v2 on v1

--- a/solution.py
+++ b/solution.py
@@ -12,14 +12,15 @@
 MESH = pl.DeviceIdType.MESH
 AXIS = "shard"
 GROUP = 16
-BATCHES = 4
-
-
-def kernel(devices, samples, x_hbm, lab_hbm, wgt_hbm, w_ref, start_ref, visit_ref,
+ORDER = (2, 1, 3, 0)
+
+
+def kernel(devices, samples, x_hbm, lab_hbm, wgt_hbm, w_hbm, start_hbm, visit_hbm,
            weights_ref, alpha_ref, objective_ref,
-           x, raw, own_lab, own_wgt, send, recv, h_all, z_all, obj_all,
-           gram, perm, onehot, onehot_t, mc, yc, cc, ac, ic, zc, zown,
-           load_sem, small_sem, own_sem, bulk_send, bulk_recv,
+           x, raw, pout, part_all, own_lab, own_wgt, w_ref, start_ref, visit_ref,
+           send, recv, h_all, z_all, obj_all,
+           gram, onehot, onehot_t, mc, yc, cc, ac, ic, zc, zown,
+           load_sem, small_sem, own_sem, bulk_send, bulk_recv, part_send, part_recv,
            rs_send, rs_recv, ag_send, ag_recv, obj_send, obj_recv):
     me = lax.axis_index(AXIS)
     local = x.shape[0]
@@ -27,21 +28,27 @@
     rows = 256
     others = devices - 1
 
-    def target(k):
-        o = lax.rem(k * 37, devices)
-        c = lax.rem(me + o, 2)
-        y = lax.rem(me // 2 + o // 2, 4)
-        xx = lax.rem(me // 8 + o // 8, 4)
-        z = lax.rem(me // 32 + o // 32, 4)
-        return ((z * 4 + xx) * 4 + y) * 2 + c
+    my_z, my_x, my_y, my_c = me // 32, lax.rem(me // 8, 4), lax.rem(me // 2, 4), lax.rem(me, 2)
+    near = [lax.rem(my_y + j // 2, 4) * 2 + lax.rem(my_c + j % 2, 2) for j in range(8)]
+
+    def peers(first, last, visit):
+        def one(i, carry):
+            base = lax.rem(my_z + i // 4, 4) * 32 + lax.rem(my_x + lax.rem(i, 4), 4) * 8
+            for j in range(8):
+                visit(base + near[j], i * 8 + j)
+            return carry
+
+        if first == 0:
+            for j in range(1, 8):
+                visit(my_z * 32 + my_x * 8 + near[j], j)
+        lax.fori_loop(max(first, 1), last, one, 0)
 
     barrier = pltpu.get_barrier_semaphore()
 
-    def greet(k, carry):
-        pl.semaphore_signal(barrier, inc=1, device_id=(target(k),), device_id_type=MESH)
-        return carry
-
-    lax.fori_loop(1, devices, greet, 0)
+    def greet(to, k):
+        pl.semaphore_signal(barrier, inc=1, device_id=(to,), device_id_type=MESH)
+
+    peers(0, 16, greet)
 
     pieces = load_sem.shape[0]
     width = samples // pieces
@@ -50,16 +57,109 @@
         at = pl.ds(i * width, width)
         return pltpu.make_async_copy(x_hbm.at[:, at], x.at[:, at], load_sem.at[i])
 
+    small = [
+        pltpu.make_async_copy(src, dst, small_sem.at[i])
+        for i, (src, dst) in enumerate(
+            (
+                (w_hbm, w_ref),
+                (lab_hbm.at[me], own_lab),
+                (wgt_hbm.at[me], own_wgt),
+                (start_hbm, start_ref),
+                (visit_hbm, visit_ref),
+            )
+        )
+    ]
+    small[0].start()
     for i in range(pieces):
         load(i).start()
-    lab_copy = pltpu.make_async_copy(lab_hbm.at[me], own_lab, small_sem.at[0])
-    wgt_copy = pltpu.make_async_copy(wgt_hbm.at[me], own_wgt, small_sem.at[1])
-    lab_copy.start()
-    wgt_copy.start()
-    own_copy = pltpu.make_async_copy(
-        x_hbm.at[:, pl.ds(pl.multiple_of(me * rows, rows), rows)], raw.at[others], own_sem
-    )
-    own_copy.start()
+    for copy in small[1:]:
+        copy.start()
+
+    def slice_of(to):
+        return pl.ds(pl.multiple_of(to * rows, rows), rows)
+
+    def group_of(line, b, yy, place, core):
+        if line == 0:
+            return ((place * 4 + lax.rem(my_x + ORDER[b], 4)) * 4 + yy) * 2 + core
+        return ((lax.rem(my_z + ORDER[b], 4) * 4 + place) * 4 + 2 + yy) * 2 + core
+
+    def collector(line, place, core):
+        if line == 0:
+            return ((place * 4 + my_x) * 4 + my_y) * 2 + core
+        return ((my_z * 4 + place) * 4 + my_y) * 2 + core
+
+    my_place = (my_z, my_x)
+
+    def own_slices(b):
+        return [
+            pltpu.make_async_copy(
+                x_hbm.at[:, slice_of(group_of(line, b, yy, my_place[line], my_c))],
+                raw.at[line, 2 * b + yy, my_place[line] * 2 + my_c],
+                own_sem.at[line, 2 * b + yy],
+            )
+            for yy in range(2)
+            for line in range(2)
+        ]
+
+    def bulk(b):
+        for yy in range(2):
+            for step, other in ((1, 0), (3, 0), (2, 1), (0, 1), (1, 1), (3, 1), (2, 0)):
+                for line in range(2):
+                    place = lax.rem(my_place[line] + step, 4)
+                    core = lax.rem(my_c + other, 2)
+                    pltpu.make_async_remote_copy(
+                        src_ref=x.at[:, slice_of(group_of(line, b, yy, place, core))],
+                        dst_ref=raw.at[line, 2 * b + yy, my_place[line] * 2 + my_c],
+                        send_sem=bulk_send.at[line, b], recv_sem=bulk_recv.at[line, b],
+                        device_id=(collector(line, place, core),), device_id_type=MESH,
+                    ).start()
+
+    def bulk_wait(b, sem):
+        for line in range(2):
+            slots = raw.at[line, pl.ds(2 * b, 2), pl.ds(0, 7)]
+            pltpu.make_async_copy(slots, slots, sem.at[line, b]).wait()
+
+    lane = lax.broadcasted_iota(jnp.int32, (128, 128), 1)
+    sub = lax.broadcasted_iota(jnp.int32, (128, 128), 0)
+
+    def partial_gram(b):
+        for copy in own_slices(b):
+            copy.wait()
+        bulk_wait(b, bulk_recv)
+        for line in range(2):
+            for yy in range(2):
+                at = line * 8 + 2 * b + yy
+                piece = raw[line, 2 * b + yy].reshape(8 * local, rows)
+                full = lax.dot_general(
+                    piece, piece, (((0,), (0,)), ((), ())), preferred_element_type=F32
+                )
+                first, last = full[:128, :128], full[128:, 128:]
+                pout[at, 0:128] = jnp.where(sub > lane, first, last).astype(BF16)
+                pout[at, 128:256] = full[128:, :128].astype(BF16)
+                diag = jnp.sum(jnp.where(sub == lane, first, 0.0), axis=0, keepdims=True)
+                pout[at, 256:272] = jnp.broadcast_to(diag, (16, 128)).astype(BF16)
+                owner = group_of(line, b, yy, my_place[line], my_c)
+                slot = (my_x, my_z)[line] * 4 + my_y
+
+                @pl.when(owner == me)
+                def _():
+                    part_all[slot] = pout[at]
+
+                @pl.when(owner != me)
+                def _():
+                    pltpu.make_async_remote_copy(
+                        src_ref=pout.at[at], dst_ref=part_all.at[slot],
+                        send_sem=part_send, recv_sem=part_recv,
+                        device_id=(owner,), device_id_type=MESH,
+                    ).start()
+
+    def partials(sem):
+        many = part_all.at[pl.ds(0, 15)]
+        pltpu.make_async_copy(many, many, sem).wait()
+
+    for b in range(4):
+        for copy in own_slices(b):
+            copy.start()
 
     eye = lax.broadcasted_iota(jnp.int32, (local, local), 0) == lax.broadcasted_iota(
         jnp.int32, (local, local), 1
@@ -71,7 +171,7 @@
     def to_col(row):
         return jnp.sum(jnp.where(eye, row, 0.0), axis=1, keepdims=True)
 
-    chunk = 2048
+    chunk = samples // 4
 
     def margins(row, phase, first, last):
         lhs = jnp.broadcast_to(row, (8, local)).astype(BF16)
@@ -90,17 +190,15 @@
         lax.fori_loop(first, last, one, 0)
 
     def scatter(phase):
-        def one(k, carry):
-            to = target(k)
+        def one(to, k):
             pltpu.make_async_remote_copy(
                 src_ref=send.at[phase, to], dst_ref=recv.at[phase, me],
                 send_sem=rs_send.at[phase], recv_sem=rs_recv.at[phase],
                 device_id=(to,), device_id_type=MESH,
             ).start()
-            return carry
 
         recv[phase, me] = send[phase, me]
-        lax.fori_loop(1, devices, one, 0)
+        peers(0, 16, one)
 
     def scattered(phase):
         many = recv.at[phase, pl.ds(0, others)]
@@ -108,37 +206,18 @@
         return jnp.sum(recv[phase], axis=0)
 
     def gather(src, buf, send_sem, recv_sem):
-        def one(k, carry):
+        def one(to, k):
             pltpu.make_async_remote_copy(
                 src_ref=src, dst_ref=buf.at[me],
                 send_sem=send_sem, recv_sem=recv_sem,
-                device_id=(target(k),), device_id_type=MESH,
+                device_id=(to,), device_id_type=MESH,
             ).start()
-            return carry
-
-        lax.fori_loop(1, devices, one, 0)
+
+        peers(0, 16, one)
 
     def drain(buf, sem):
         many = buf.at[pl.ds(0, others)]
         pltpu.make_async_copy(many, many, sem).wait()
-
-    def bulk(batch):
-        def one(k, carry):
-            to = target(k)
-            pltpu.make_async_remote_copy(
-                src_ref=x.at[:, pl.ds(pl.multiple_of(to * rows, rows), rows)],
-                dst_ref=raw.at[k - 1],
-                send_sem=bulk_send.at[batch], recv_sem=bulk_recv.at[batch],
-                device_id=(to,), device_id_type=MESH,
-            ).start()
-            return carry
-
-        size = devices // BATCHES
-        lax.fori_loop(batch * size + 1, min((batch + 1) * size, others) + 1, one, 0)
-
-    def batch_slots(batch):
-        size = devices // BATCHES
-        return raw.at[pl.ds(batch * size, min((batch + 1) * size, others) - batch * size)]
 
     def contract(buf):
         def one(d, acc):
@@ -149,6 +228,7 @@
         acc = lax.fori_loop(0, devices, one, jnp.zeros((local, 128), F32), unroll=4)
         return jnp.sum(acc, axis=1, keepdims=True)
 
+    small[0].wait()
     w_row = w_ref[...]
     per = width // chunk
     for i in range(pieces):
@@ -164,8 +244,8 @@
 
     sq = lax.fori_loop(0, devices, square, jnp.zeros((local, 128), F32), unroll=4)
     scale = jnp.sum(sq, axis=1, keepdims=True) / samples + 1e-06
-    lab_copy.wait()
-    wgt_copy.wait()
+    for copy in small[1:]:
+        copy.wait()
     sign = own_lab[...].astype(F32)
     bound = own_wgt[...]
 
@@ -174,8 +254,6 @@
     gather(h_all.at[me], h_all, ag_send.at[0], ag_recv.at[0])
     bulk(1)
     alpha0 = bound * start_ref[...]
-    lane = lax.broadcasted_iota(jnp.int32, (128, 128), 1)
-    sub = lax.broadcasted_iota(jnp.int32, (128, 128), 0)
 
     def permuted(vec, b):
         col = jnp.sum(onehot[b] * vec[b : b + 1], axis=1, keepdims=True)
@@ -191,6 +269,7 @@
         cc[part] = permuted(bound, b)
         ac[part] = permuted(alpha0, b)
 
+    partial_gram(0)
     drain(h_all, ag_recv.at[0])
     w_col = to_col(w_row)
     stepped = w_col + contract(h_all) / (samples * scale)
@@ -199,45 +278,40 @@
     penalty = jnp.sum(jnp.abs(primal)) / (4.0 * features)
     margins(to_row(primal), 1, 0, samples // chunk)
     scatter(1)
-    for batch in range(2, BATCHES):
-        bulk(batch)
+    bulk(2)
+    bulk(3)
+    partial_gram(1)
     v1 = scattered(1)
     loss = jnp.sum(bound * jnp.square(jnp.maximum(0.0, 1.0 - sign * v1))) / (2.0 * samples)
     obj_all[me] = jnp.full((1, 128), loss + penalty, F32)
 
-    own_copy.wait()
-    gram[...] = jnp.zeros_like(gram)
-    size = devices // BATCHES
-    for batch in range(BATCHES):
-        slots = batch_slots(batch)
-        pltpu.make_async_copy(slots, slots, bulk_recv.at[batch]).wait()
-
-        def one(i, carry):
-            piece = raw[pl.ds(batch * size + i * 16, 16)].reshape(16 * local, rows)
-            gram[...] += lax.dot_general(
-                piece, piece, (((0,), (0,)), ((), ())), preferred_element_type=F32
-            )
-            return carry
-
-        lax.fori_loop(0, size // 16, one, 0)
+    partial_gram(2)
+    partial_gram(3)
+    partials(part_recv)
 
     def halves(a):
         hi = a.astype(BF16)
         return hi, (a - hi.astype(F32)).astype(BF16)
 
-    for b in range(2):
-        cols = slice(128 * b, 128 * b + 128)
-        hi, lo = halves(gram[:, cols])
-        perm[:, cols] = jnp.dot(hi, onehot_t[b], preferred_element_type=F32) + jnp.dot(
-            lo, onehot_t[b], preferred_element_type=F32
+    def reordered(a, b1, b2):
+        hi, lo = halves(a)
+        mid = jnp.dot(hi, onehot_t[b2], preferred_element_type=F32) + jnp.dot(
+            lo, onehot_t[b2], preferred_element_type=F32
         )
-    for b in range(2):
-        part = slice(128 * b, 128 * b + 128)
-        left = onehot[b].astype(BF16)
-        hi, lo = halves(perm[part, :])
-        gram[part, :] = jnp.dot(left, hi, preferred_element_type=F32) + jnp.dot(
+        hi, lo = halves(mid)
+        left = onehot[b1].astype(BF16)
+        return jnp.dot(left, hi, preferred_element_type=F32) + jnp.dot(
             left, lo, preferred_element_type=F32
         )
+
+    packed = jnp.sum(part_all[:, 0:128].astype(F32), axis=0)
+    turned = jnp.transpose(packed)
+    diag_row = jnp.sum(part_all[:, 256:272].astype(F32), axis=0)[0:1]
+    first_block = jnp.where(sub > lane, packed, jnp.where(sub < lane, turned, diag_row))
+    last_block = jnp.where(sub > lane, turned, packed)
+    gram[0:128, 0:128] = reordered(first_block, 0, 0)
+    gram[128:256, 0:128] = reordered(jnp.sum(part_all[:, 128:256].astype(F32), axis=0), 1, 0)
+    gram[128:256, 128:256] = reordered(last_block, 1, 1)
     for b in range(2):
         part = slice(128 * b, 128 * b + 128)
         diag = jnp.sum(jnp.where(lane == sub, gram[part, part], 0.0), axis=1, keepdims=True)
@@ -294,9 +368,9 @@
     drain(h_all, ag_send.at[0])
     drain(z_all.at[0], ag_send.at[1])
     drain(obj_all, obj_send)
-    for batch in range(BATCHES):
-        slots = batch_slots(batch)
-        pltpu.make_async_copy(slots, slots, bulk_send.at[batch]).wait()
+    for b in range(4):
+        bulk_wait(b, bulk_send)
+    partials(part_send)
     drain(z_all.at[1], ag_recv.at[2])
     second_dw = contract(z_all.at[1]) * (2.0 / devices)
     weights_ref[...] = to_row(primal + first_dw + second_dw)
@@ -320,25 +394,29 @@
                 jax.ShapeDtypeStruct((2, 128), F32),
                 jax.ShapeDtypeStruct((1, 128), F32),
             ),
-            in_specs=[anyspace, anyspace, anyspace, vmem, vmem, vmem],
+            in_specs=[anyspace] * 6,
             out_specs=(vmem, vmem, vmem),
             scratch_shapes=[
                 pltpu.VMEM((local, samples), BF16),
-                pltpu.VMEM((devices, local, per), BF16),
+                pltpu.VMEM((2, 8, 8, local, per), BF16),
+                pltpu.VMEM((16, 272, 128), BF16),
+                pltpu.VMEM((16, 272, 128), BF16),
                 pltpu.VMEM((2, 128), jnp.int32),
                 pltpu.VMEM((2, 128), F32),
+                pltpu.VMEM((1, local), F32),
+                pltpu.VMEM((2, 128), F32),
+                pltpu.VMEM((2, 128), jnp.int32),
                 pltpu.VMEM((3, devices, 2, 128), F32),
                 pltpu.VMEM((3, devices, 2, 128), F32),
                 pltpu.VMEM((devices, 2, 128), BF16),
                 pltpu.VMEM((2, devices, 2, 128), BF16),
                 pltpu.VMEM((devices, 1, 128), F32),
                 pltpu.VMEM((per, per), F32),
-                pltpu.VMEM((per, per), F32),
                 pltpu.VMEM((2, 128, 128), F32),
                 pltpu.VMEM((2, 128, 128), BF16),
                 square, square, square, square, square, square,
                 pltpu.VMEM((2, 128), F32),
-                dma((8,)), dma((2,)), dma, dma((BATCHES,)), dma((BATCHES,)),
+                dma((4,)), dma((5,)), dma((2, 8)), dma((2, 4)), dma((2, 4)), dma, dma,
                 dma((3,)), dma((3,)), dma((3,)), dma((3,)), dma, dma,
             ],
             compiler_params=pltpu.CompilerParams(collective_id=0, has_side_effects=True),

time: 123 us -> 88.8 us (0.72)
  Pallas kernels: 118 us -> 83.8 us
    pallas_call x1, Pallas kernels: 118 us -> 83.8 us  [body(): pl.pallas_call(functools.partial(kernel, devices, samples), out_shape=(ja...]
where the time goes in v2:
time: 88.8 us; the launch traced here: 88.6 us
  Pallas kernels  83.8 us (94%)
  between operations  2.4 us (3%)
  local copies, waits for them, and re-layouts  2.36 us (3%)
    pallas_call x1, Pallas kernels, body(): pl.pallas_call(functools.partial(kernel, devices, samples), out_shape=(ja...  83.8 us
    unnamed x2, local copies, waits for them, and re-layouts  2.36 us

profile of v2, /device:TPU:1, one launch (start us, length us, event | category | flops | bytes accessed | tf_op | source)
XLA Modules:
  0.0 88.6 jit_solution(16737046727313114982)
XLA Ops:
  0.6 83.8 %shard_map.85 = (f32[1,64]{1,0:T(1,128)}, f32[2,128]{1,0:T(2,128)}, f32[1,128]{1,0:T(1,128)}) custom-call(bf16[64,32768]{1,0:T(8,128)(2,1)} %x_hbm.1, s32[128,2,128]{2,1,0:T(2,128)} %bitcast.8, f32[128,2,128]{2,1,0:T(2,128)} %bitcast.9, f32[1,64]{1,0:T(1,128)} %bitcast.12, f32[2,128]{1,0:T(2,128)} %bitcast.10, s32[2,128]{1,0:T(2,128)} %visit_hbm.1), custom_call_target="tpu_custom_call" | custom-call | tf_op jit(solution)/shard_map/pallas_call | solution.py:390
  84.5 1.1 %copy.12 = f32[64]{0:T(128)} copy(f32[64]{0:T(128)} %bitcast.14) | data formatting | bytes 512
  85.6 1.2 %copy.13 = f32[256]{0:T(256)} copy(f32[256]{0:T(256)} %bitcast.11) | data formatting | bytes 2048

commit v3 on v2

--- a/solution.py
+++ b/solution.py
@@ -17,10 +17,10 @@
 
 def kernel(devices, samples, x_hbm, lab_hbm, wgt_hbm, w_hbm, start_hbm, visit_hbm,
            weights_ref, alpha_ref, objective_ref,
-           x, raw, pout, part_all, own_lab, own_wgt, w_ref, start_ref, visit_ref,
+           x, raw, pout, mid, psum, fin, own_sum, own_lab, own_wgt, w_ref, start_ref, visit_ref,
            send, recv, h_all, z_all, obj_all,
            gram, onehot, onehot_t, mc, yc, cc, ac, ic, zc, zown,
-           load_sem, small_sem, own_sem, bulk_send, bulk_recv, part_send, part_recv,
+           load_sem, small_sem, own_sem, bulk_send, bulk_recv, mid_send, mid_recv, fin_send, fin_recv,
            rs_send, rs_recv, ag_send, ag_recv, obj_send, obj_recv):
     me = lax.axis_index(AXIS)
     local = x.shape[0]
@@ -29,26 +29,30 @@
     others = devices - 1
 
     my_z, my_x, my_y, my_c = me // 32, lax.rem(me // 8, 4), lax.rem(me // 2, 4), lax.rem(me, 2)
-    near = [lax.rem(my_y + j // 2, 4) * 2 + lax.rem(my_c + j % 2, 2) for j in range(8)]
-
-    def peers(first, last, visit):
+    near = [
+        lax.rem(my_y + dy, 4) * 2 + lax.rem(my_c + dc, 2)
+        for dy in (2, 1, 3, 0)
+        for dc in (1, 0)
+    ]
+
+    def peers(visit):
         def one(i, carry):
-            base = lax.rem(my_z + i // 4, 4) * 32 + lax.rem(my_x + lax.rem(i, 4), 4) * 8
-            for j in range(8):
-                visit(base + near[j], i * 8 + j)
+            base = (
+                lax.rem(my_z + 2 + i // 4, 4) * 32 + lax.rem(my_x + 2 + lax.rem(i, 4), 4) * 8
+            )
+            for place in near:
+                visit(base + place)
             return carry
 
-        if first == 0:
-            for j in range(1, 8):
-                visit(my_z * 32 + my_x * 8 + near[j], j)
-        lax.fori_loop(max(first, 1), last, one, 0)
+        lax.fori_loop(0, 10, one, 0)
+        lax.fori_loop(11, 16, one, 0)
+        for place in near[:7]:
+            visit(my_z * 32 + my_x * 8 + place)
 
     barrier = pltpu.get_barrier_semaphore()
 
-    def greet(to, k):
+    def greet(to):
         pl.semaphore_signal(barrier, inc=1, device_id=(to,), device_id_type=MESH)
-
-    peers(0, 16, greet)
 
     pieces = load_sem.shape[0]
     width = samples // pieces
@@ -72,6 +76,7 @@
     small[0].start()
     for i in range(pieces):
         load(i).start()
+    peers(greet)
     for copy in small[1:]:
         copy.start()
 
@@ -122,40 +127,47 @@
     lane = lax.broadcasted_iota(jnp.int32, (128, 128), 1)
     sub = lax.broadcasted_iota(jnp.int32, (128, 128), 0)
 
+    def to_row_owner(b, dy):
+        y = lax.rem(my_y + dy, 4)
+        return pltpu.make_async_remote_copy(
+            src_ref=pout.at[b, y], dst_ref=mid.at[b, dy - 1],
+            send_sem=mid_send.at[b], recv_sem=mid_recv.at[b],
+            device_id=((my_z * 4 + my_x) * 8 + y * 2 + my_c,), device_id_type=MESH,
+        )
+
     def partial_gram(b):
         for copy in own_slices(b):
             copy.wait()
         bulk_wait(b, bulk_recv)
         for line in range(2):
             for yy in range(2):
-                at = line * 8 + 2 * b + yy
+                at = line * 2 + yy
                 piece = raw[line, 2 * b + yy].reshape(8 * local, rows)
                 full = lax.dot_general(
                     piece, piece, (((0,), (0,)), ((), ())), preferred_element_type=F32
                 )
                 first, last = full[:128, :128], full[128:, 128:]
-                pout[at, 0:128] = jnp.where(sub > lane, first, last).astype(BF16)
-                pout[at, 128:256] = full[128:, :128].astype(BF16)
+                pout[b, at, 0:128] = jnp.where(sub > lane, first, last).astype(BF16)
+                pout[b, at, 128:256] = full[128:, :128].astype(BF16)
                 diag = jnp.sum(jnp.where(sub == lane, first, 0.0), axis=0, keepdims=True)
-                pout[at, 256:272] = jnp.broadcast_to(diag, (16, 128)).astype(BF16)
-                owner = group_of(line, b, yy, my_place[line], my_c)
-                slot = (my_x, my_z)[line] * 4 + my_y
-
-                @pl.when(owner == me)
-                def _():
-                    part_all[slot] = pout[at]
-
-                @pl.when(owner != me)
-                def _():
-                    pltpu.make_async_remote_copy(
-                        src_ref=pout.at[at], dst_ref=part_all.at[slot],
-                        send_sem=part_send, recv_sem=part_recv,
-                        device_id=(owner,), device_id_type=MESH,
-                    ).start()
-
-    def partials(sem):
-        many = part_all.at[pl.ds(0, 15)]
-        pltpu.make_async_copy(many, many, sem).wait()
+                pout[b, at, 256:272] = jnp.broadcast_to(diag, (16, 128)).astype(BF16)
+        for dy in (2, 1, 3):
+            to_row_owner(b, dy).start()
+
+    def middle(b):
+        pltpu.make_async_copy(mid.at[b], mid.at[b], mid_recv.at[b]).wait()
+        total = pout[b, my_y].astype(F32) + jnp.sum(mid[b].astype(F32), axis=0)
+        if ORDER[b] == 0:
+            own_sum[...] = total
+        else:
+            line = my_y // 2
+            z = lax.rem(my_z + ORDER[b] * line, 4)
+            xx = lax.rem(my_x + ORDER[b] * (1 - line), 4)
+            psum[b] = total.astype(BF16)
+            pltpu.make_async_remote_copy(
+                src_ref=psum.at[b], dst_ref=fin.at[b], send_sem=fin_send, recv_sem=fin_recv,
+                device_id=((z * 4 + xx) * 8 + my_y * 2 + my_c,), device_id_type=MESH,
+            ).start()
 
     for b in range(4):
         for copy in own_slices(b):
@@ -190,7 +202,7 @@
         lax.fori_loop(first, last, one, 0)
 
     def scatter(phase):
-        def one(to, k):
+        def one(to):
             pltpu.make_async_remote_copy(
                 src_ref=send.at[phase, to], dst_ref=recv.at[phase, me],
                 send_sem=rs_send.at[phase], recv_sem=rs_recv.at[phase],
@@ -198,7 +210,7 @@
             ).start()
 
         recv[phase, me] = send[phase, me]
-        peers(0, 16, one)
+        peers(one)
 
     def scattered(phase):
         many = recv.at[phase, pl.ds(0, others)]
@@ -206,14 +218,14 @@
         return jnp.sum(recv[phase], axis=0)
 
     def gather(src, buf, send_sem, recv_sem):
-        def one(to, k):
+        def one(to):
             pltpu.make_async_remote_copy(
                 src_ref=src, dst_ref=buf.at[me],
                 send_sem=send_sem, recv_sem=recv_sem,
                 device_id=(to,), device_id_type=MESH,
             ).start()
 
-        peers(0, 16, one)
+        peers(one)
 
     def drain(buf, sem):
         many = buf.at[pl.ds(0, others)]
@@ -253,6 +265,7 @@
     h_all[me] = (bound * sign * jnp.maximum(0.0, 1.0 - sign * v0)).astype(BF16)
     gather(h_all.at[me], h_all, ag_send.at[0], ag_recv.at[0])
     bulk(1)
+    bulk(2)
     alpha0 = bound * start_ref[...]
 
     def permuted(vec, b):
@@ -278,16 +291,19 @@
     penalty = jnp.sum(jnp.abs(primal)) / (4.0 * features)
     margins(to_row(primal), 1, 0, samples // chunk)
     scatter(1)
-    bulk(2)
     bulk(3)
     partial_gram(1)
+    middle(0)
     v1 = scattered(1)
     loss = jnp.sum(bound * jnp.square(jnp.maximum(0.0, 1.0 - sign * v1))) / (2.0 * samples)
     obj_all[me] = jnp.full((1, 128), loss + penalty, F32)
 
     partial_gram(2)
+    middle(1)
     partial_gram(3)
-    partials(part_recv)
+    middle(2)
+    middle(3)
+    pltpu.make_async_copy(fin, fin, fin_recv).wait()
 
     def halves(a):
         hi = a.astype(BF16)
@@ -304,13 +320,16 @@
             left, lo, preferred_element_type=F32
         )
 
-    packed = jnp.sum(part_all[:, 0:128].astype(F32), axis=0)
+    def whole(first, last):
+        return own_sum[first:last] + jnp.sum(fin[:, first:last].astype(F32), axis=0)
+
+    packed = whole(0, 128)
     turned = jnp.transpose(packed)
-    diag_row = jnp.sum(part_all[:, 256:272].astype(F32), axis=0)[0:1]
+    diag_row = whole(256, 272)[0:1]
     first_block = jnp.where(sub > lane, packed, jnp.where(sub < lane, turned, diag_row))
     last_block = jnp.where(sub > lane, turned, packed)
     gram[0:128, 0:128] = reordered(first_block, 0, 0)
-    gram[128:256, 0:128] = reordered(jnp.sum(part_all[:, 128:256].astype(F32), axis=0), 1, 0)
+    gram[128:256, 0:128] = reordered(whole(128, 256), 1, 0)
     gram[128:256, 128:256] = reordered(last_block, 1, 1)
     for b in range(2):
         part = slice(128 * b, 128 * b + 128)
@@ -370,7 +389,8 @@
     drain(obj_all, obj_send)
     for b in range(4):
         bulk_wait(b, bulk_send)
-    partials(part_send)
+        pltpu.make_async_copy(mid.at[b], mid.at[b], mid_send.at[b]).wait()
+    pltpu.make_async_copy(fin, fin, fin_send).wait()
     drain(z_all.at[1], ag_recv.at[2])
     second_dw = contract(z_all.at[1]) * (2.0 / devices)
     weights_ref[...] = to_row(primal + first_dw + second_dw)
@@ -399,8 +419,11 @@
             scratch_shapes=[
                 pltpu.VMEM((local, samples), BF16),
                 pltpu.VMEM((2, 8, 8, local, per), BF16),
-                pltpu.VMEM((16, 272, 128), BF16),
-                pltpu.VMEM((16, 272, 128), BF16),
+                pltpu.VMEM((4, 4, 272, 128), BF16),
+                pltpu.VMEM((4, 3, 272, 128), BF16),
+                pltpu.VMEM((3, 272, 128), BF16),
+                pltpu.VMEM((3, 272, 128), BF16),
+                pltpu.VMEM((272, 128), F32),
                 pltpu.VMEM((2, 128), jnp.int32),
                 pltpu.VMEM((2, 128), F32),
                 pltpu.VMEM((1, local), F32),
@@ -416,7 +439,7 @@
                 pltpu.VMEM((2, 128, 128), BF16),
                 square, square, square, square, square, square,
                 pltpu.VMEM((2, 128), F32),
-                dma((4,)), dma((5,)), dma((2, 8)), dma((2, 4)), dma((2, 4)), dma, dma,
+                dma((4,)), dma((5,)), dma((2, 8)), dma((2, 4)), dma((2, 4)), dma((4,)), dma((4,)), dma, dma,
                 dma((3,)), dma((3,)), dma((3,)), dma((3,)), dma, dma,
             ],
             compiler_params=pltpu.CompilerParams(collective_id=0, has_side_effects=True),

time: 88.8 us -> 77.2 us (0.87)
  Pallas kernels: 83.8 us -> 72.3 us
    pallas_call x1, Pallas kernels: 83.8 us -> 72.3 us  [body(): pl.pallas_call(functools.partial(kernel, devices, samples), out_shape=(ja...]
where the time goes in v3:
time: 77.2 us; the launch traced here: 77.1 us
  Pallas kernels  72.3 us (94%)
  between operations  2.4 us (3%)
  local copies, waits for them, and re-layouts  2.36 us (3%)
    pallas_call x1, Pallas kernels, body(): pl.pallas_call(functools.partial(kernel, devices, samples), out_shape=(ja...  72.3 us
    unnamed x2, local copies, waits for them, and re-layouts  2.36 us

profile of v3, /device:TPU:1, one launch (start us, length us, event | category | flops | bytes accessed | tf_op | source)
XLA Modules:
  0.0 77.1 jit_solution(9585414228091484153)
XLA Ops:
  0.6 72.3 %shard_map.85 = (f32[1,64]{1,0:T(1,128)}, f32[2,128]{1,0:T(2,128)}, f32[1,128]{1,0:T(1,128)}) custom-call(bf16[64,32768]{1,0:T(8,128)(2,1)} %x_hbm.1, s32[128,2,128]{2,1,0:T(2,128)} %bitcast.8, f32[128,2,128]{2,1,0:T(2,128)} %bitcast.9, f32[1,64]{1,0:T(1,128)} %bitcast.12, f32[2,128]{1,0:T(2,128)} %bitcast.10, s32[2,128]{1,0:T(2,128)} %visit_hbm.1), custom_call_target="tpu_custom_call" | custom-call | tf_op jit(solution)/shard_map/pallas_call | solution.py:410
  73.0 1.1 %copy.12 = f32[64]{0:T(128)} copy(f32[64]{0:T(128)} %bitcast.14) | data formatting | bytes 512
  74.1 1.2 %copy.13 = f32[256]{0:T(256)} copy(f32[256]{0:T(256)} %bitcast.11) | data formatting | bytes 2048

commit v4 on v3

--- a/solution.py
+++ b/solution.py
@@ -16,10 +16,10 @@
 
 
 def kernel(devices, samples, x_hbm, lab_hbm, wgt_hbm, w_hbm, start_hbm, visit_hbm,
-           weights_ref, alpha_ref, objective_ref,
+           result_ref,
            x, raw, pout, mid, psum, fin, own_sum, own_lab, own_wgt, w_ref, start_ref, visit_ref,
            send, recv, h_all, z_all, obj_all,
-           gram, onehot, onehot_t, mc, yc, cc, ac, ic, zc, zown,
+           gram, onehot, onehot_t, mc, yc, lc, cc, ac, ic, zc, zown,
            load_sem, small_sem, own_sem, bulk_send, bulk_recv, mid_send, mid_recv, fin_send, fin_recv,
            rs_send, rs_recv, ag_send, ag_recv, obj_send, obj_recv):
     me = lax.axis_index(AXIS)
@@ -83,93 +83,125 @@
     def slice_of(to):
         return pl.ds(pl.multiple_of(to * rows, rows), rows)
 
-    def group_of(line, b, yy, place, core):
-        if line == 0:
-            return ((place * 4 + lax.rem(my_x + ORDER[b], 4)) * 4 + yy) * 2 + core
-        return ((lax.rem(my_z + ORDER[b], 4) * 4 + place) * 4 + 2 + yy) * 2 + core
+    def device(z, xx, y, core):
+        return ((z * 4 + xx) * 4 + y) * 2 + core
+
+    def line_of(entry):
+        return entry % 3 if entry < 12 else (entry - 12) // 2
+
+    def owner_of(entry, place, core):
+        line = line_of(entry)
+        if entry >= 12:
+            y = entry - 12
+            other = lax.rem(11 - place - y, 4)
+            return device(place, other, y, core) if line == 0 else device(other, place, y, core)
+        away = ORDER[entry // 3]
+        if line == 2:
+            z = lax.rem(my_z + away, 4)
+            return device(z, lax.rem(10 - z - place, 4), place, core)
+        y = lax.rem(my_y + away, 4)
+        other = lax.rem(8 + line - place - y, 4)
+        return device(place, other, y, core) if line == 0 else device(other, place, y, core)
 
     def collector(line, place, core):
-        if line == 0:
-            return ((place * 4 + my_x) * 4 + my_y) * 2 + core
-        return ((my_z * 4 + place) * 4 + my_y) * 2 + core
-
-    my_place = (my_z, my_x)
+        at = [my_z, my_x, my_y]
+        at[line] = place
+        return device(*at, core)
+
+    my_place = (my_z, my_x, my_y)
+
+    def entries(b):
+        return range(12, 16) if b == 4 else range(3 * b, 3 * b + 3)
 
     def own_slices(b):
         return [
             pltpu.make_async_copy(
-                x_hbm.at[:, slice_of(group_of(line, b, yy, my_place[line], my_c))],
-                raw.at[line, 2 * b + yy, my_place[line] * 2 + my_c],
-                own_sem.at[line, 2 * b + yy],
+                x_hbm.at[:, slice_of(owner_of(e, my_place[line_of(e)], my_c))],
+                raw.at[e, my_place[line_of(e)] * 2 + my_c],
+                own_sem.at[e],
             )
-            for yy in range(2)
-            for line in range(2)
+            for e in entries(b)
         ]
 
     def bulk(b):
-        for yy in range(2):
-            for step, other in ((1, 0), (3, 0), (2, 1), (0, 1), (1, 1), (3, 1), (2, 0)):
-                for line in range(2):
-                    place = lax.rem(my_place[line] + step, 4)
-                    core = lax.rem(my_c + other, 2)
-                    pltpu.make_async_remote_copy(
-                        src_ref=x.at[:, slice_of(group_of(line, b, yy, place, core))],
-                        dst_ref=raw.at[line, 2 * b + yy, my_place[line] * 2 + my_c],
-                        send_sem=bulk_send.at[line, b], recv_sem=bulk_recv.at[line, b],
-                        device_id=(collector(line, place, core),), device_id_type=MESH,
-                    ).start()
+        for step, other in ((1, 0), (3, 0), (2, 1), (0, 1), (1, 1), (3, 1), (2, 0)):
+            for e in entries(b):
+                line = line_of(e)
+                place = lax.rem(my_place[line] + step, 4)
+                core = lax.rem(my_c + other, 2)
+                pltpu.make_async_remote_copy(
+                    src_ref=x.at[:, slice_of(owner_of(e, place, core))],
+                    dst_ref=raw.at[e, my_place[line] * 2 + my_c],
+                    send_sem=bulk_send.at[b], recv_sem=bulk_recv.at[b],
+                    device_id=(collector(line, place, core),), device_id_type=MESH,
+                ).start()
 
     def bulk_wait(b, sem):
-        for line in range(2):
-            slots = raw.at[line, pl.ds(2 * b, 2), pl.ds(0, 7)]
-            pltpu.make_async_copy(slots, slots, sem.at[line, b]).wait()
+        part = entries(b)
+        slots = raw.at[pl.ds(part[0], len(part)), pl.ds(0, 7)]
+        pltpu.make_async_copy(slots, slots, sem.at[b]).wait()
 
     lane = lax.broadcasted_iota(jnp.int32, (128, 128), 1)
     sub = lax.broadcasted_iota(jnp.int32, (128, 128), 0)
 
-    def to_row_owner(b, dy):
-        y = lax.rem(my_y + dy, 4)
-        return pltpu.make_async_remote_copy(
-            src_ref=pout.at[b, y], dst_ref=mid.at[b, dy - 1],
-            send_sem=mid_send.at[b], recv_sem=mid_recv.at[b],
-            device_id=((my_z * 4 + my_x) * 8 + y * 2 + my_c,), device_id_type=MESH,
-        )
+    def push(entry, j, slot, z, y):
+        pltpu.make_async_remote_copy(
+            src_ref=pout.at[entry], dst_ref=mid.at[j, slot],
+            send_sem=mid_send.at[j], recv_sem=mid_recv.at[j],
+            device_id=(device(z, my_x, y, my_c),), device_id_type=MESH,
+        ).start()
 
     def partial_gram(b):
         for copy in own_slices(b):
             copy.wait()
         bulk_wait(b, bulk_recv)
-        for line in range(2):
-            for yy in range(2):
-                at = line * 2 + yy
-                piece = raw[line, 2 * b + yy].reshape(8 * local, rows)
-                full = lax.dot_general(
-                    piece, piece, (((0,), (0,)), ((), ())), preferred_element_type=F32
-                )
-                first, last = full[:128, :128], full[128:, 128:]
-                pout[b, at, 0:128] = jnp.where(sub > lane, first, last).astype(BF16)
-                pout[b, at, 128:256] = full[128:, :128].astype(BF16)
-                diag = jnp.sum(jnp.where(sub == lane, first, 0.0), axis=0, keepdims=True)
-                pout[b, at, 256:272] = jnp.broadcast_to(diag, (16, 128)).astype(BF16)
-        for dy in (2, 1, 3):
-            to_row_owner(b, dy).start()
-
-    def middle(b):
-        pltpu.make_async_copy(mid.at[b], mid.at[b], mid_recv.at[b]).wait()
-        total = pout[b, my_y].astype(F32) + jnp.sum(mid[b].astype(F32), axis=0)
-        if ORDER[b] == 0:
+        for e in entries(b):
+            piece = raw[e].reshape(8 * local, rows)
+            full = lax.dot_general(
+                piece, piece, (((0,), (0,)), ((), ())), preferred_element_type=F32
+            )
+            first, last = full[:128, :128], full[128:, 128:]
+            pout[e, 0:128] = jnp.where(sub > lane, first, last).astype(BF16)
+            pout[e, 128:256] = full[128:, :128].astype(BF16)
+            diag = jnp.sum(jnp.where(sub == lane, first, 0.0), axis=0, keepdims=True)
+            pout[e, 256:272] = jnp.broadcast_to(diag, (16, 128)).astype(BF16)
+            if e < 9:
+                away = ORDER[e // 3]
+                if line_of(e) == 2:
+                    push(e, 2, e // 3, lax.rem(my_z + away, 4), my_y)
+                else:
+                    push(e, line_of(e), e // 3, my_z, lax.rem(my_y + away, 4))
+        if b == 4:
+            for dy in (2, 1, 3):
+                y = lax.rem(my_y + dy, 4)
+                push(12 + y, 3, dy - 1, my_z, y)
+
+    def middle(j):
+        pltpu.make_async_copy(mid.at[j], mid.at[j], mid_recv.at[j]).wait()
+        own = pout[9 + j] if j < 3 else pout[12 + my_y]
+        total = own.astype(F32) + jnp.sum(mid[j].astype(F32), axis=0)
+        along_x = lax.rem(8 + j - my_z - my_y, 4)
+        along_z = lax.rem(8 + j - my_x - my_y, 4)
+        turn = {0: 0, 1: 1, 2: 0, 3: my_y // 2}[j]
+        z = my_z * (1 - turn) + along_z * turn
+        xx = along_x * (1 - turn) + my_x * turn
+        slot = lax.rem(z - my_z + xx - my_x + 4, 4) - 1
+        mine = lax.rem(my_z + my_x + my_y, 4) == j
+
+        @pl.when(mine)
+        def _():
             own_sum[...] = total
-        else:
-            line = my_y // 2
-            z = lax.rem(my_z + ORDER[b] * line, 4)
-            xx = lax.rem(my_x + ORDER[b] * (1 - line), 4)
-            psum[b] = total.astype(BF16)
+
+        @pl.when(jnp.logical_not(mine))
+        def _():
+            psum[j] = total.astype(BF16)
             pltpu.make_async_remote_copy(
-                src_ref=psum.at[b], dst_ref=fin.at[b], send_sem=fin_send, recv_sem=fin_recv,
-                device_id=((z * 4 + xx) * 8 + my_y * 2 + my_c,), device_id_type=MESH,
+                src_ref=psum.at[j], dst_ref=fin.at[slot],
+                send_sem=fin_send, recv_sem=fin_recv,
+                device_id=(device(z, xx, my_y, my_c),), device_id_type=MESH,
             ).start()
 
-    for b in range(4):
+    for b in (4, 0, 1, 2, 3):
         for copy in own_slices(b):
             copy.start()
 
@@ -248,7 +280,9 @@
         margins(w_row, 0, i * per, (i + 1) * per)
     pl.semaphore_wait(barrier, others)
     scatter(0)
+    bulk(4)
     bulk(0)
+    bulk(1)
 
     def square(d, acc):
         part = x[:, pl.ds(pl.multiple_of(d * rows, rows), rows)].astype(F32)
@@ -264,8 +298,8 @@
     v0 = scattered(0)
     h_all[me] = (bound * sign * jnp.maximum(0.0, 1.0 - sign * v0)).astype(BF16)
     gather(h_all.at[me], h_all, ag_send.at[0], ag_recv.at[0])
-    bulk(1)
     bulk(2)
+    bulk(3)
     alpha0 = bound * start_ref[...]
 
     def permuted(vec, b):
@@ -279,10 +313,14 @@
     for b in range(2):
         part = slice(128 * b, 128 * b + 128)
         yc[part] = permuted(sign, b)
-        cc[part] = permuted(bound, b)
-        ac[part] = permuted(alpha0, b)
-
+        edge = yc[part] * permuted(bound, b)
+        lc[part] = jnp.minimum(edge, 0.0)
+        cc[part] = jnp.maximum(edge, 0.0)
+        ac[part] = yc[part] * permuted(alpha0, b)
+
+    partial_gram(4)
     partial_gram(0)
+    partial_gram(1)
     drain(h_all, ag_recv.at[0])
     w_col = to_col(w_row)
     stepped = w_col + contract(h_all) / (samples * scale)
@@ -291,18 +329,16 @@
     penalty = jnp.sum(jnp.abs(primal)) / (4.0 * features)
     margins(to_row(primal), 1, 0, samples // chunk)
     scatter(1)
-    bulk(3)
-    partial_gram(1)
+    partial_gram(2)
+    partial_gram(3)
+    middle(3)
     middle(0)
+    middle(1)
+    middle(2)
     v1 = scattered(1)
     loss = jnp.sum(bound * jnp.square(jnp.maximum(0.0, 1.0 - sign * v1))) / (2.0 * samples)
     obj_all[me] = jnp.full((1, 128), loss + penalty, F32)
 
-    partial_gram(2)
-    middle(1)
-    partial_gram(3)
-    middle(2)
-    middle(3)
     pltpu.make_async_copy(fin, fin, fin_recv).wait()
 
     def halves(a):
@@ -341,18 +377,20 @@
 
     def sweep(margin):
         for b in range(2):
-            mc[128 * b : 128 * b + 128] = permuted(margin, b)
+            part = slice(128 * b, 128 * b + 128)
+            mc[part] = ac[part] + (yc[part] - permuted(margin, b)) * ic[part]
         c = [jnp.zeros((1, 128), F32), jnp.zeros((1, 128), F32)]
         for t in range(rows // GROUP):
             at = slice(GROUP * t, GROUP * t + GROUP)
             b, first = t // 8, GROUP * (t % 8)
-            prod = gram[at, 0:128] * c[0]
-            if b:
-                prod = prod + gram[at, 128:256] * c[1]
-            m = mc[at] + 2.0 * jnp.sum(prod, axis=1, keepdims=True)
-            old, y = ac[at], yc[at]
-            new = jnp.clip(old + (1.0 - y * m) * ic[at], 0.0, cc[at])
-            step = y * (new - old)
+            aim = mc[at]
+            if t:
+                prod = gram[at, 0:128] * c[0]
+                if b:
+                    prod = prod + gram[at, 128:256] * c[1]
+                aim = aim - 2.0 * ic[at] * jnp.sum(prod, axis=1, keepdims=True)
+            new = jnp.minimum(jnp.maximum(aim, lc[at]), cc[at])
+            step = new - ac[at]
             ac[at] = new
             zc[at] = step
             c[b] = c[b] + jnp.sum(
@@ -379,22 +417,29 @@
     z_all[1, me] = zown[...].astype(BF16)
     gather(z_all.at[1, me], z_all.at[1], ag_send.at[2], ag_recv.at[2])
     for b in range(2):
-        alpha_ref[b : b + 1] = natural(ac, b)
+        result_ref[1 + b : 2 + b] = sign[b : b + 1] * natural(ac, b)
     drain(obj_all, obj_recv)
-    objective_ref[...] = jnp.sum(obj_all[...], axis=0)
+    result_ref[3:4] = jnp.sum(obj_all[...], axis=0)
     for phase in range(3):
         drain(send.at[phase], rs_send.at[phase])
     drain(h_all, ag_send.at[0])
     drain(z_all.at[0], ag_send.at[1])
     drain(obj_all, obj_send)
-    for b in range(4):
+    for b in range(5):
         bulk_wait(b, bulk_send)
-        pltpu.make_async_copy(mid.at[b], mid.at[b], mid_send.at[b]).wait()
+    for j in range(4):
+        pltpu.make_async_copy(mid.at[j], mid.at[j], mid_send.at[j]).wait()
     pltpu.make_async_copy(fin, fin, fin_send).wait()
     drain(z_all.at[1], ag_recv.at[2])
     second_dw = contract(z_all.at[1]) * (2.0 / devices)
-    weights_ref[...] = to_row(primal + first_dw + second_dw)
+    result_ref[0:1, :local] = to_row(primal + first_dw + second_dw)
     drain(z_all.at[1], ag_send.at[2])
+
+
+def finish(result, weights, alpha, objective):
+    weights[...] = result[0:1, : weights.shape[1]]
+    alpha[...] = result[1:3]
+    objective[...] = result[3:4]
 
 
 def solution(mesh):
@@ -407,21 +452,17 @@
         vmem = pl.BlockSpec(memory_space=pltpu.VMEM)
         square = pltpu.VMEM((per, 128), F32)
         dma = pltpu.SemaphoreType.DMA
-        weights, alpha, objective = pl.pallas_call(
+        result = pl.pallas_call(
             functools.partial(kernel, devices, samples),
-            out_shape=(
-                jax.ShapeDtypeStruct((1, local), F32),
-                jax.ShapeDtypeStruct((2, 128), F32),
-                jax.ShapeDtypeStruct((1, 128), F32),
-            ),
+            out_shape=jax.ShapeDtypeStruct((4, 128), F32),
             in_specs=[anyspace] * 6,
-            out_specs=(vmem, vmem, vmem),
+            out_specs=vmem,
             scratch_shapes=[
                 pltpu.VMEM((local, samples), BF16),
-                pltpu.VMEM((2, 8, 8, local, per), BF16),
-                pltpu.VMEM((4, 4, 272, 128), BF16),
+                pltpu.VMEM((16, 8, local, per), BF16),
+                pltpu.VMEM((16, 272, 128), BF16),
                 pltpu.VMEM((4, 3, 272, 128), BF16),
-                pltpu.VMEM((3, 272, 128), BF16),
+                pltpu.VMEM((4, 272, 128), BF16),
                 pltpu.VMEM((3, 272, 128), BF16),
                 pltpu.VMEM((272, 128), F32),
                 pltpu.VMEM((2, 128), jnp.int32),
@@ -437,12 +478,14 @@
                 pltpu.VMEM((per, per), F32),
                 pltpu.VMEM((2, 128, 128), F32),
                 pltpu.VMEM((2, 128, 128), BF16),
-                square, square, square, square, square, square,
+                *[square] * 7,
                 pltpu.VMEM((2, 128), F32),
-                dma((4,)), dma((5,)), dma((2, 8)), dma((2, 4)), dma((2, 4)), dma((4,)), dma((4,)), dma, dma,
+                dma((4,)), dma((5,)), dma((16,)), dma((5,)), dma((5,)), dma((4,)), dma((4,)), dma, dma,
                 dma((3,)), dma((3,)), dma((3,)), dma((3,)), dma, dma,
             ],
-            compiler_params=pltpu.CompilerParams(collective_id=0, has_side_effects=True),
+            compiler_params=pltpu.CompilerParams(
+                collective_id=0, has_side_effects=True, vmem_limit_bytes=61998 * 1024
+            ),
         )(
             data_t,
             labels.reshape(devices, 2, 128),
@@ -451,6 +494,17 @@
             alpha_start.reshape(2, 128),
             visit_order,
         )
+        weights, alpha, objective = pl.pallas_call(
+            finish,
+            out_shape=(
+                jax.ShapeDtypeStruct((1, local), F32),
+                jax.ShapeDtypeStruct((2, 128), F32),
+                jax.ShapeDtypeStruct((1, 128), F32),
+            ),
+            in_specs=[vmem],
+            out_specs=(vmem,) * 3,
+            compiler_params=pltpu.CompilerParams(vmem_limit_bytes=1024 * 1024),
+        )(result)
         return weights.reshape(local), alpha.reshape(per), objective[0, 0]
 
     return jax.shard_map(

time: 77.2 us -> 71.8 us (0.930)
  Pallas kernels: 72.3 us -> 70.4 us
  between operations: 2.4 us -> 0.65 us
  local copies, waits for them, and re-layouts: 2.36 us -> 0.65 us
    pallas_call x1 -> x2, Pallas kernels: 72.3 us -> 70.4 us  [the longest x1 69.8 us: body(): pl.pallas_call(functools.partial(kernel, devices, samples), out_shape=jax...]
    unnamed x2, local copies, waits for them, and re-layouts: 2.36 us -> 0.65 us
where the time goes in v4:
time: 71.8 us; the launch traced here: 71.7 us
  Pallas kernels  70.4 us (98%)
    pallas_call x1, Pallas kernels, body(): pl.pallas_call(functools.partial(kernel, devices, samples), out_shape=jax...  69.8 us

profile of v4, /device:TPU:1, one launch (start us, length us, event | category | flops | bytes accessed | tf_op | source)
XLA Modules:
  0.0 71.7 jit_solution(17042040495547538268)
XLA Ops:
  0.6 69.8 %shard_map.85.result = f32[4,128]{1,0:T(4,128)} custom-call(bf16[64,32768]{1,0:T(8,128)(2,1)} %x_hbm.1, s32[128,2,128]{2,1,0:T(2,128)} %bitcast.8, f32[128,2,128]{2,1,0:T(2,128)} %bitcast.9, f32[1,64]{1,0:T(1,128)} %bitcast.11, f32[2,128]{1,0:T(2,128)} %bitcast.10, s32[2,128]{1,0:T(2,128)} %visit_hbm.1), custom_call_target="tpu_custom_call" | custom-call | tf_op jit(solution)/shard_map/pallas_call | solution.py:455
  70.5 0.0 copy-start
  70.5 0.6 copy-done
  71.1 0.6 shard_map.86
Async XLA Ops:
  70.5 0.7 copy-start

commit v5 on v4

--- a/solution.py
+++ b/solution.py
@@ -35,19 +35,26 @@
         for dc in (1, 0)
     ]
 
+    def plane(dz, visit):
+        z = lax.rem(my_z + dz, 4)
+
+        def one(dx, carry):
+            for place in near:
+                visit(z * 32 + lax.rem(my_x + dx, 4) * 8 + place)
+            return carry
+
+        if dz:
+            lax.fori_loop(2, 6, one, 0)
+        else:
+            lax.fori_loop(1, 4, one, 0)
+            for place in near[:7]:
+                visit(z * 32 + my_x * 8 + place)
+
+    PLANES = (2, 1, 3, 0)
+
     def peers(visit):
-        def one(i, carry):
-            base = (
-                lax.rem(my_z + 2 + i // 4, 4) * 32 + lax.rem(my_x + 2 + lax.rem(i, 4), 4) * 8
-            )
-            for place in near:
-                visit(base + place)
-            return carry
-
-        lax.fori_loop(0, 10, one, 0)
-        lax.fori_loop(11, 16, one, 0)
-        for place in near[:7]:
-            visit(my_z * 32 + my_x * 8 + place)
+        for dz in PLANES:
+            plane(dz, visit)
 
     barrier = pltpu.get_barrier_semaphore()
 
@@ -233,7 +240,7 @@
 
         lax.fori_loop(first, last, one, 0)
 
-    def scatter(phase):
+    def scatter(phase, before):
         def one(to):
             pltpu.make_async_remote_copy(
                 src_ref=send.at[phase, to], dst_ref=recv.at[phase, me],
@@ -241,8 +248,13 @@
                 device_id=(to,), device_id_type=MESH,
             ).start()
 
+        for dz in PLANES:
+            before(lax.rem(my_z + dz, 4))
+            plane(dz, one)
         recv[phase, me] = send[phase, me]
-        peers(one)
+
+    def margins_scatter(row, phase):
+        scatter(phase, lambda z: margins(row, phase, z, z + 1))
 
     def scattered(phase):
         many = recv.at[phase, pl.ds(0, others)]
@@ -250,26 +262,38 @@
         return jnp.sum(recv[phase], axis=0)
 
     def gather(src, buf, send_sem, recv_sem):
-        def one(to):
-            pltpu.make_async_remote_copy(
-                src_ref=src, dst_ref=buf.at[me],
-                send_sem=send_sem, recv_sem=recv_sem,
-                device_id=(to,), device_id_type=MESH,
-            ).start()
-
-        peers(one)
+        for dz in PLANES:
+
+            def one(to):
+                pltpu.make_async_remote_copy(
+                    src_ref=src, dst_ref=buf.at[me],
+                    send_sem=send_sem, recv_sem=recv_sem.at[dz],
+                    device_id=(to,), device_id_type=MESH,
+                ).start()
+
+            plane(dz, one)
+
+    def arrived(buf, sem, dz):
+        many = buf.at[pl.ds(0, devices // 4 - (dz == 0))]
+        pltpu.make_async_copy(many, many, sem.at[dz]).wait()
 
     def drain(buf, sem):
         many = buf.at[pl.ds(0, others)]
         pltpu.make_async_copy(many, many, sem).wait()
 
-    def contract(buf):
-        def one(d, acc):
-            part = x[:, pl.ds(pl.multiple_of(d * rows, rows), rows)].astype(F32)
-            v = buf[d].astype(F32)
-            return acc + part[:, :128] * v[0:1] + part[:, 128:] * v[1:2]
-
-        acc = lax.fori_loop(0, devices, one, jnp.zeros((local, 128), F32), unroll=4)
+    def contract(buf, sem):
+        acc = jnp.zeros((local, 128), F32)
+        for dz in PLANES[::-1]:
+            arrived(buf, sem, dz)
+            first = lax.rem(my_z + 4 - dz, 4) * 32
+
+            def one(i, acc):
+                d = first + i
+                part = x[:, pl.ds(pl.multiple_of(d * rows, rows), rows)].astype(F32)
+                v = buf[d].astype(F32)
+                return acc + part[:, :128] * v[0:1] + part[:, 128:] * v[1:2]
+
+            acc = lax.fori_loop(0, 32, one, acc, unroll=4)
         return jnp.sum(acc, axis=1, keepdims=True)
 
     small[0].wait()
@@ -279,7 +303,7 @@
         load(i).wait()
         margins(w_row, 0, i * per, (i + 1) * per)
     pl.semaphore_wait(barrier, others)
-    scatter(0)
+    scatter(0, lambda z: None)
     bulk(4)
     bulk(0)
     bulk(1)
@@ -321,14 +345,12 @@
     partial_gram(4)
     partial_gram(0)
     partial_gram(1)
-    drain(h_all, ag_recv.at[0])
     w_col = to_col(w_row)
-    stepped = w_col + contract(h_all) / (samples * scale)
+    stepped = w_col + contract(h_all, ag_recv.at[0]) / (samples * scale)
     thresh = 1.0 / (4.0 * features * scale)
     primal = stepped - jnp.clip(stepped, -thresh, thresh)
     penalty = jnp.sum(jnp.abs(primal)) / (4.0 * features)
-    margins(to_row(primal), 1, 0, samples // chunk)
-    scatter(1)
+    margins_scatter(to_row(primal), 1)
     partial_gram(2)
     partial_gram(3)
     middle(3)
@@ -406,10 +428,8 @@
     z_all[0, me] = zown[...].astype(BF16)
     gather(z_all.at[0, me], z_all.at[0], ag_send.at[1], ag_recv.at[1])
     gather(obj_all.at[me], obj_all, obj_send, obj_recv)
-    drain(z_all.at[0], ag_recv.at[1])
-    first_dw = contract(z_all.at[0]) * (2.0 / devices)
-    margins(to_row(first_dw), 2, 0, samples // chunk)
-    scatter(2)
+    first_dw = contract(z_all.at[0], ag_recv.at[1]) * (2.0 / devices)
+    margins_scatter(to_row(first_dw), 2)
     v2 = v1 + scattered(2)
     sweep(v2)
     for b in range(2):
@@ -418,7 +438,8 @@
     gather(z_all.at[1, me], z_all.at[1], ag_send.at[2], ag_recv.at[2])
     for b in range(2):
         result_ref[1 + b : 2 + b] = sign[b : b + 1] * natural(ac, b)
-    drain(obj_all, obj_recv)
+    for dz in PLANES:
+        arrived(obj_all, obj_recv, dz)
     result_ref[3:4] = jnp.sum(obj_all[...], axis=0)
     for phase in range(3):
         drain(send.at[phase], rs_send.at[phase])
@@ -430,8 +451,7 @@
     for j in range(4):
         pltpu.make_async_copy(mid.at[j], mid.at[j], mid_send.at[j]).wait()
     pltpu.make_async_copy(fin, fin, fin_send).wait()
-    drain(z_all.at[1], ag_recv.at[2])
-    second_dw = contract(z_all.at[1]) * (2.0 / devices)
+    second_dw = contract(z_all.at[1], ag_recv.at[2]) * (2.0 / devices)
     result_ref[0:1, :local] = to_row(primal + first_dw + second_dw)
     drain(z_all.at[1], ag_send.at[2])
 
@@ -481,7 +501,7 @@
                 *[square] * 7,
                 pltpu.VMEM((2, 128), F32),
                 dma((4,)), dma((5,)), dma((16,)), dma((5,)), dma((5,)), dma((4,)), dma((4,)), dma, dma,
-                dma((3,)), dma((3,)), dma((3,)), dma((3,)), dma, dma,
+                dma((3,)), dma((3,)), dma((3,)), dma((3, 4)), dma, dma((4,)),
             ],
             compiler_params=pltpu.CompilerParams(
                 collective_id=0, has_side_effects=True, vmem_limit_bytes=61998 * 1024

time: 71.8 us -> 68.9 us (0.960)
  Pallas kernels: 70.4 us -> 67.5 us
    pallas_call x1, Pallas kernels: 69.8 us -> 66.9 us  [body(): pl.pallas_call(functools.partial(kernel, devices, samples), out_shape=jax...]
where the time goes in v5:
time: 68.9 us; the launch traced here: 68.8 us
  Pallas kernels  67.5 us (98%)
    pallas_call x1, Pallas kernels, body(): pl.pallas_call(functools.partial(kernel, devices, samples), out_shape=jax...  66.9 us

profile of v5, /device:TPU:1, one launch (start us, length us, event | category | flops | bytes accessed | tf_op | source)
XLA Modules:
  0.0 68.8 jit_solution(15087167987793565162)
XLA Ops:
  0.6 66.9 %shard_map.85.result = f32[4,128]{1,0:T(4,128)} custom-call(bf16[64,32768]{1,0:T(8,128)(2,1)} %x_hbm.1, s32[128,2,128]{2,1,0:T(2,128)} %bitcast.8, f32[128,2,128]{2,1,0:T(2,128)} %bitcast.9, f32[1,64]{1,0:T(1,128)} %bitcast.11, f32[2,128]{1,0:T(2,128)} %bitcast.10, s32[2,128]{1,0:T(2,128)} %visit_hbm.1), custom_call_target="tpu_custom_call" | custom-call | tf_op jit(solution)/shard_map/pallas_call | solution.py:475
  67.6 0.0 copy-start
  67.6 0.6 copy-done
  68.2 0.6 shard_map.86
Async XLA Ops:
  67.6 0.7 copy-start

commit v6 on v5

--- a/solution.py
+++ b/solution.py
@@ -345,18 +345,18 @@
     partial_gram(4)
     partial_gram(0)
     partial_gram(1)
+    partial_gram(2)
     w_col = to_col(w_row)
     stepped = w_col + contract(h_all, ag_recv.at[0]) / (samples * scale)
     thresh = 1.0 / (4.0 * features * scale)
     primal = stepped - jnp.clip(stepped, -thresh, thresh)
     penalty = jnp.sum(jnp.abs(primal)) / (4.0 * features)
     margins_scatter(to_row(primal), 1)
-    partial_gram(2)
     partial_gram(3)
     middle(3)
+    middle(2)
+    middle(1)
     middle(0)
-    middle(1)
-    middle(2)
     v1 = scattered(1)
     loss = jnp.sum(bound * jnp.square(jnp.maximum(0.0, 1.0 - sign * v1))) / (2.0 * samples)
     obj_all[me] = jnp.full((1, 128), loss + penalty, F32)

time: 68.9 us -> 67.3 us (0.977)
  Pallas kernels: 67.5 us -> 65.9 us
    pallas_call x1, Pallas kernels: 66.9 us -> 65.3 us  [body(): pl.pallas_call(functools.partial(kernel, devices, samples), out_shape=jax...]
where the time goes in v6:
time: 67.3 us; the launch traced here: 67.2 us
  Pallas kernels  65.9 us (98%)
    pallas_call x1, Pallas kernels, body(): pl.pallas_call(functools.partial(kernel, devices, samples), out_shape=jax...  65.3 us

profile of v6, /device:TPU:1, one launch (start us, length us, event | category | flops | bytes accessed | tf_op | source)
XLA Modules:
  0.0 67.2 jit_solution(12304302274570764128)
XLA Ops:
  0.6 65.3 %shard_map.85.result = f32[4,128]{1,0:T(4,128)} custom-call(bf16[64,32768]{1,0:T(8,128)(2,1)} %x_hbm.1, s32[128,2,128]{2,1,0:T(2,128)} %bitcast.8, f32[128,2,128]{2,1,0:T(2,128)} %bitcast.9, f32[1,64]{1,0:T(1,128)} %bitcast.11, f32[2,128]{1,0:T(2,128)} %bitcast.10, s32[2,128]{1,0:T(2,128)} %visit_hbm.1), custom_call_target="tpu_custom_call" | custom-call | tf_op jit(solution)/shard_map/pallas_call | solution.py:475
  65.9 0.0 copy-start
  66.0 0.6 copy-done
  66.6 0.6 shard_map.86
Async XLA Ops:
  65.9 0.7 copy-start

commit v7 on v6

--- a/solution.py
+++ b/solution.py
@@ -104,8 +104,8 @@
             return device(place, other, y, core) if line == 0 else device(other, place, y, core)
         away = ORDER[entry // 3]
         if line == 2:
-            z = lax.rem(my_z + away, 4)
-            return device(z, lax.rem(10 - z - place, 4), place, core)
+            xx = lax.rem(my_x + away, 4)
+            return device(lax.rem(10 - xx - place, 4), xx, place, core)
         y = lax.rem(my_y + away, 4)
         other = lax.rem(8 + line - place - y, 4)
         return device(place, other, y, core) if line == 0 else device(other, place, y, core)
@@ -151,11 +151,11 @@
     lane = lax.broadcasted_iota(jnp.int32, (128, 128), 1)
     sub = lax.broadcasted_iota(jnp.int32, (128, 128), 0)
 
-    def push(entry, j, slot, z, y):
+    def push(entry, j, slot, xx, y):
         pltpu.make_async_remote_copy(
             src_ref=pout.at[entry], dst_ref=mid.at[j, slot],
             send_sem=mid_send.at[j], recv_sem=mid_recv.at[j],
-            device_id=(device(z, my_x, y, my_c),), device_id_type=MESH,
+            device_id=(device(my_z, xx, y, my_c),), device_id_type=MESH,
         ).start()
 
     def partial_gram(b):
@@ -175,13 +175,13 @@
             if e < 9:
                 away = ORDER[e // 3]
                 if line_of(e) == 2:
-                    push(e, 2, e // 3, lax.rem(my_z + away, 4), my_y)
+                    push(e, 2, e // 3, lax.rem(my_x + away, 4), my_y)
                 else:
-                    push(e, line_of(e), e // 3, my_z, lax.rem(my_y + away, 4))
+                    push(e, line_of(e), e // 3, my_x, lax.rem(my_y + away, 4))
         if b == 4:
             for dy in (2, 1, 3):
                 y = lax.rem(my_y + dy, 4)
-                push(12 + y, 3, dy - 1, my_z, y)
+                push(12 + y, 3, dy - 1, my_x, y)
 
     def middle(j):
         pltpu.make_async_copy(mid.at[j], mid.at[j], mid_recv.at[j]).wait()
@@ -189,7 +189,7 @@
         total = own.astype(F32) + jnp.sum(mid[j].astype(F32), axis=0)
         along_x = lax.rem(8 + j - my_z - my_y, 4)
         along_z = lax.rem(8 + j - my_x - my_y, 4)
-        turn = {0: 0, 1: 1, 2: 0, 3: my_y // 2}[j]
+        turn = {0: 0, 1: 1, 2: 1, 3: my_y // 2}[j]
         z = my_z * (1 - turn) + along_z * turn
         xx = along_x * (1 - turn) + my_x * turn
         slot = lax.rem(z - my_z + xx - my_x + 4, 4) - 1

time: 67.3 us -> 67.3 us (level)
  no operation moved by 1% of the time
where the time goes in v7:
time: 67.3 us; the launch traced here: 67.2 us
  Pallas kernels  65.9 us (98%)
    pallas_call x1, Pallas kernels, body(): pl.pallas_call(functools.partial(kernel, devices, samples), out_shape=jax...  65.3 us

profile of v7, /device:TPU:1, one launch (start us, length us, event | category | flops | bytes accessed | tf_op | source)
XLA Modules:
  0.0 67.2 jit_solution(15027021219572513301)
XLA Ops:
  0.6 65.3 %shard_map.85.result = f32[4,128]{1,0:T(4,128)} custom-call(bf16[64,32768]{1,0:T(8,128)(2,1)} %x_hbm.1, s32[128,2,128]{2,1,0:T(2,128)} %bitcast.8, f32[128,2,128]{2,1,0:T(2,128)} %bitcast.9, f32[1,64]{1,0:T(1,128)} %bitcast.11, f32[2,128]{1,0:T(2,128)} %bitcast.10, s32[2,128]{1,0:T(2,128)} %visit_hbm.1), custom_call_target="tpu_custom_call" | custom-call | tf_op jit(solution)/shard_map/pallas_call | solution.py:475
  65.9 0.0 copy-start
  66.0 0.6 copy-done
  66.6 0.6 shard_map.86
Async XLA Ops:
  65.9 0.7 copy-start
